TPU v7x, 256 devices: a whole 4x4x8 slice. The times are simulated.
256 devices in a mesh: seq: 64 (over z, y, core), hid: 4 (over x).
Axes of the slice: x: 4, y: 4, z: 8, core: 2. Of those that a mesh axis runs over, the one named last changes fastest.
Arguments:
- gate_half: bfloat16 [8192, 2048], P('seq', 'hid'), may hold values from -6 to 6
- value_half: bfloat16 [8192, 2048], P('seq', 'hid'), may hold values from -6 to 6
- norm_gain: float32 [2048], P('hid'), may hold values from 0.25 to 1.75
- norm_shift: float32 [2048], P('hid'), may hold values from -0.5 to 0.5
- token_weight: bfloat16 [8192, 8192], P('seq'), may hold values from -0.1875 to 0.1875
- token_bias: float32 [8192], P('seq'), may hold values from 0.5 to 1.5
- grad_output: bfloat16 [8192, 2048], P('seq', 'hid'), may hold values from -6 to 6
Outputs:
- grad_gate: bfloat16 [8192, 2048], P('seq', 'hid')
- grad_value: bfloat16 [8192, 2048], P('seq', 'hid')
- grad_gain: float32 [2048], P('hid')
- grad_shift: float32 [2048], P('hid')
- grad_weight: float32 [8192, 8192], P('seq', 'hid')
- grad_token_bias: float32 [8192], P('seq')
All inputs are finite; a program needn't handle non-finite values.
Results may differ from a plain program's by a relative error of at most 0.005.
Values may be sent and summed in bfloat16 or wider, within the bound.
A program may use at most 64 MiB of HBM per device.

v0:
```python
import jax
import jax.numpy as jnp
from jax import lax
from jax.sharding import PartitionSpec as P

HIDDEN_SIZE = 2048


def sent_to_all(array, axis):
    copies = jnp.broadcast_to(array, (lax.axis_size(axis), *array.shape))
    return lax.all_to_all(copies, axis, split_axis=0, concat_axis=0, tiled=True)


def taken_together(array, axis):
    everything = sent_to_all(array, axis)
    return jnp.sum(everything, axis=0)


def packed_total(arrays, axis):
    flat, at, gathered = (jnp.concatenate([a.reshape(-1) for a in arrays]), 0, [])
    subtotal = taken_together(flat, axis)
    for a in arrays:
        gathered.append(subtotal[at : at + a.size].reshape(a.shape))
        at += a.size
    return tuple(gathered)


def per_device(gate_half, value_half, norm_gain, norm_shift, token_weight, token_bias, grad_output):
    local_rows = gate_half.shape[0]
    channels = gate_half.shape[1]
    all_tokens = token_weight.shape[1]
    row_start = lax.axis_index("seq") * local_rows
    row_last = row_start + local_rows - 1
    row_ids = row_start + lax.iota(jnp.int32, local_rows)[:, None]
    second = value_half.astype(jnp.float32)
    upstream = grad_output.astype(jnp.float32)
    grad_mix = (upstream * gate_half.astype(jnp.float32)).astype(jnp.bfloat16)
    sum_first, sum_square, grad_token_bias = lax.psum(
        (
            jnp.sum(second, axis=1),
            jnp.sum(second * second, axis=1),
            jnp.sum(grad_mix.astype(jnp.float32), axis=1),
        ),
        "hid",
    )
    row_mean = (sum_first / HIDDEN_SIZE)[:, None]
    row_var = (sum_square / HIDDEN_SIZE)[:, None] - row_mean * row_mean
    inv_std = lax.rsqrt(row_var + 1e-05)
    centred = (second - row_mean) * inv_std
    normed = (centred * norm_gain + norm_shift).astype(jnp.bfloat16)
    start_pair = (
        jnp.zeros((local_rows, channels), jnp.float32),
        jnp.zeros((local_rows, all_tokens), jnp.float32),
    )
    shard_rows = lax.all_gather(normed, "seq", axis=0, tiled=True)
    length = shard_rows.shape[0]

    def compute(pair):
        weight_block = token_weight
        column_ids = lax.iota(jnp.int32, length)[None, :]
        lower_mask = column_ids <= row_ids
        weight_block = jnp.where(lower_mask, weight_block, jnp.zeros_like(weight_block))
        mixed_sum = jnp.dot(weight_block, shard_rows, preferred_element_type=jnp.float32)
        outer = jnp.einsum("tc,nc->tn", grad_mix, shard_rows, preferred_element_type=jnp.float32)
        outer = jnp.where(lower_mask, outer, 0.0)
        return (mixed_sum, outer)

    mixed_sum, weight_term = lax.cond(
        jnp.int32(0) <= row_last, compute, lambda pair: pair, start_pair
    )
    spatial = mixed_sum + token_bias[:, None]
    grad_gate = (upstream * spatial).astype(jnp.bfloat16)
    grad_weight = lax.psum_scatter(weight_term, "hid", scatter_dimension=1, tiled=True)
    columns = lax.all_to_all(token_weight, "seq", split_axis=1, concat_axis=0, tiled=True)
    own_ids = row_start + lax.iota(jnp.int32, local_rows)[None, :]
    fold_shard_rows = lax.all_gather(grad_mix, "seq", axis=0, tiled=True)
    fold_length = fold_shard_rows.shape[0]

    def compute(running):
        weight_block = columns
        source_ids = lax.iota(jnp.int32, fold_length)[:, None]
        weight_block = jnp.where(source_ids >= own_ids, weight_block, jnp.zeros_like(weight_block))
        return jnp.einsum(
            "nt,nc->tc", weight_block, fold_shard_rows, preferred_element_type=jnp.float32
        )

    grad_normed = lax.cond(
        jnp.int32(0) + fold_length - 1 >= row_start,
        compute,
        lambda running: running,
        jnp.zeros((local_rows, channels), jnp.float32),
    )
    grad_gain, grad_shift = packed_total(
        (jnp.sum(grad_normed * centred, axis=0), jnp.sum(grad_normed, axis=0)), "seq"
    )
    grad_centred = grad_normed * norm_gain
    sum_grad, sum_cross = lax.psum(
        (jnp.sum(grad_centred, axis=1), jnp.sum(grad_centred * centred, axis=1)), "hid"
    )
    first_mean = (sum_grad / HIDDEN_SIZE)[:, None]
    second_mean = (sum_cross / HIDDEN_SIZE)[:, None]
    grad_value = (inv_std * (grad_centred - first_mean - centred * second_mean)).astype(
        jnp.bfloat16
    )
    return (grad_gate, grad_value, grad_gain, grad_shift, grad_weight, grad_token_bias)


def solution(mesh):
    placed = (
        P("seq", "hid"),
        P("seq", "hid"),
        P("hid"),
        P("hid"),
        P("seq", None),
        P("seq"),
        P("seq", "hid"),
    )
    return jax.shard_map(
        per_device,
        mesh=mesh,
        in_specs=placed,
        out_specs=(P("seq", "hid"), P("seq", "hid"), P("hid"), P("hid"), P("seq", "hid"), P("seq")),
        check_vma=False,
    )
```

profile of v0, /device:TPU:1, one launch (start us, length us, event | category | flops | bytes accessed | tf_op | source)
XLA Modules:
  0.0 270.6 jit_solution(11396971279304036208)
XLA Ops:
  7.2 0.0 all-gather.5.cloned.1.call-start
  7.2 1.7 convert_reduce_fusion.1
  8.9 0.0 all-gather.5.cloned.1.call-update
  8.9 0.0 copy-start.3
  8.9 4.1 %copy.17 = bf16[128,8192]{0,1:T(8,128)(2,1)} copy(bf16[128,8192]{1,0:T(8,128)(2,1)} %param.15) | data formatting | bytes 4194304 | tf_op args[4]
  13.0 13.1 %all-to-all-start = ((bf16[128,64,128]{0,2,1:T(8,128)(2,1)}), bf16[128,64,128]{0,2,1:T(8,128)(2,1)S(1)}, u32[]{:S(2)}, u32[]{:S(2)}) async-start(bf16[128,64,128]{0,2,1:T(8,128)(2,1)} %bitcast.13), calls=%async_computation | async-start | bytes 4194304 | tf_op jit(solution)/shard_map/all_to_all | solution.py:74
  26.2 0.0 all-gather.3.cloned.1.call-start
  26.2 0.1 convert_reduce_fusion
  26.4 9.1 %all-reduce.1 = (f32[128]{0:T(128)S(1)}, f32[128]{0:T(128)S(1)}) all-reduce(f32[128]{0:T(128)S(1)} %get-tuple-element.62, f32[128]{0:T(128)S(1)} %get-tuple-element.61), channel_id=1, replica_groups=mesh['seq'=64,'hid'=4] {'hid'}, use_global_device_ids=true, to_apply=%region_3.0 | all-reduce | flops 256 | bytes 2048 | tf_op jit(solution)/shard_map/psum | solution.py:38
  35.5 48.1 %all-to-all-done = bf16[128,64,128]{0,2,1:T(8,128)(2,1)S(1)} async-done(((bf16[128,64,128]{0,2,1:T(8,128)(2,1)}), bf16[128,64,128]{0,2,1:T(8,128)(2,1)S(1)}, u32[]{:S(2)}, u32[]{:S(2)}) %all-to-all-start) | async-done | bytes 2097184 | tf_op jit(solution)/shard_map/all_to_all | solution.py:74
  83.6 23.1 %all-gather.5.cloned.1.call-done = bf16[8192,512]{1,0:T(8,128)(2,1)} async-done(((bf16[128,512]{1,0:T(8,128)(2,1)}), bf16[8192,512]{1,0:T(8,128)(2,1)}) %all-gather.5.cloned.1.call-update) | async-done | bytes 8388624 | tf_op jit(solution)/shard_map/all_gather | solution.py:76
  106.7 9.3 %conditional.3 = (f32[128,512]{1,0:T(8,128)S(1)}) conditional(s32[]{:T(128)} %convert_element_type.37, () %tuple.24, (s32[]{:T(128)}, s32[1,128]{1,0:T(1,128)S(1)}, bf16[64,128,128]{1,2,0:T(8,128)(2,1)S(1)}, bf16[8192,512]{1,0:T(8,128)(2,1)}) %tuple.49), branch_computations={%region_6.0_spmd, %region_7.8_spmd} | conditional | flops 1075839104 | bytes 23332392 | solution.py:87
  106.7 1.4 copy-done.1
  108.1 3.2 %copy.18 = bf16[64,128,128]{2,1,0:T(8,128)(2,1)S(1)} copy(bf16[64,128,128]{1,2,0:T(8,128)(2,1)} %copy-done.1) | data formatting | bytes 4194304 | tf_op jit(solution)/shard_map
  111.3 4.7 %fusion.7 = f32[128,512]{1,0:T(8,128)S(1)} fusion(bf16[8192,512]{1,0:T(8,128)(2,1)} %get-tuple-element.34, bf16[8192,128]{1,0:T(8,128)(2,1)S(1)} %bitcast.11, s32[128]{0:T(128)S(1)} %add_bitcast_fusion.1), kind=kOutput, calls=%fused_computation.10 | convolution fusion | flops 1075838976 | bytes 10748416 | tf_op jit(solution)/shard_map/cond/branch_1_fun/nt,nc->tc/dot_general | solution.py:83
  116.0 0.2 fusion.25
  116.2 9.0 %all-reduce = (f32[128]{0:T(128)S(1)}, f32[128]{0:T(128)S(1)}, f32[128]{0:T(128)}) all-reduce(f32[128]{0:T(128)S(1)} %get-tuple-element.58, f32[128]{0:T(128)S(1)} %get-tuple-element.59, f32[128]{0:T(128)S(1)} %get-tuple-element.68), channel_id=1, replica_groups=mesh['seq'=64,'hid'=4] {'hid'}, use_global_device_ids=true, to_apply=%region_11.12 | all-reduce | flops 384 | bytes 3072 | tf_op jit(solution)/shard_map/psum | solution.py:97
  125.2 0.9 fusion.24
  126.1 0.0 all-gather.3.cloned.1.call-update
  126.1 0.0 reduce-scatter.2.cloned.1.call-start
  126.2 80.8 %all-gather.3.cloned.1.call-done = bf16[8192,512]{1,0:T(8,128)(2,1)} async-done(((bf16[128,512]{1,0:T(8,128)(2,1)}), bf16[8192,512]{1,0:T(8,128)(2,1)}) %all-gather.3.cloned.1.call-update) | async-done | bytes 8388624 | tf_op jit(solution)/shard_map/all_gather | solution.py:55
  207.0 11.2 %conditional.2 = (f32[128,512]{1,0:T(8,128)S(1)}, f32[128,8192]{1,0:T(8,128)}) conditional(s32[]{:T(128)} %convert_element_type.31, () %tuple.22, (s32[]{:T(128)}, s32[128,1]{0,1:T(1,128)S(1)}, bf16[128,8192]{1,0:T(8,128)(2,1)}, bf16[8192,512]{1,0:T(8,128)(2,1)}, bf16[128,512]{1,0:T(8,128)(2,1)S(1)}) %tuple.50), branch_computations={%region_4.0_spmd, %region_5.0_spmd} | conditional | flops 2151677952 | bytes 57018416 | solution.py:68
  207.0 5.4 %fusion.1 = f32[128,512]{1,0:T(8,128)S(1)} fusion(bf16[8192,512]{1,0:T(8,128)(2,1)} %get-tuple-element.29, bf16[128,8192]{1,0:T(8,128)(2,1)} %get-tuple-element.28, s32[128]{0:T(128)S(1)} %add_bitcast_fusion), kind=kOutput, calls=%fused_computation.3 | convolution fusion | flops 1075838976 | bytes 10748416 | tf_op jit(solution)/shard_map/cond/branch_1_fun/dot_general | solution.py:63
  212.5 0.9 copy-done
  213.4 4.8 %convolution_select_fusion = f32[128,8192]{1,0:T(8,128)} fusion(bf16[128,512]{1,0:T(8,128)(2,1)S(1)} %get-tuple-element.30, bf16[8192,512]{1,0:T(8,128)(2,1)S(1)} %copy-done, s32[128]{0:T(128)S(1)} %add_bitcast_fusion), kind=kOutput, calls=%fused_computation | convolution fusion | flops 1075838976 | bytes 12714496 | tf_op jit(solution)/shard_map/cond/branch_1_fun/tc,nc->tn/dot_general | solution.py:64
  218.2 0.0 reduce-scatter.2.cloned.1.call-update
  218.2 0.1 broadcast_in_dim.8
  218.4 18.7 %all_to_all.25 = f32[64,1,1024]{2,1,0:T(1,128)S(1)} all-to-all(f32[64,1,1024]{2,1,0:T(1,128)S(1)} %broadcast_in_dim.8), channel_id=1, replica_groups=mesh['seq'=64,'hid'=4] {'seq'}, dimensions={0} | all-to-all | bytes 524288 | tf_op jit(solution)/shard_map/all_to_all | solution.py:11
  237.1 0.2 reduce_sum.78
  237.2 0.6 fusion.28
  237.8 0.8 fusion.13
  238.6 25.5 %reduce-scatter.2.cloned.1.call-done = f32[128,2048]{1,0:T(8,128)} async-done(((f32[128,8192]{1,0:T(8,128)}), f32[128,2048]{1,0:T(8,128)}) %reduce-scatter.2.cloned.1.call-update) | async-done | bytes 1048592 | tf_op jit(solution)/shard_map/reduce_scatter | solution.py:73
  (20 shorter events, 0.1 us)
Async XLA Ops:
  7.2 99.5 %all-gather.5.cloned.1.call-start = ((), (), s32[]{:S(2)}) async-start(), calls=%async_computation.4 | async-start | bytes 8519680 | tf_op jit(solution)/shard_map/all_gather | solution.py:76
  8.9 17.3 %copy-start.3 = (bf16[128,512]{1,0:T(8,128)(2,1)S(1)}, bf16[128,512]{1,0:T(8,128)(2,1)}, u32[]{:S(2)}) copy-start(bf16[128,512]{1,0:T(8,128)(2,1)} %param.12) | copy-start | bytes 393220
  13.0 70.6 %all-to-all-start = ((bf16[128,64,128]{0,2,1:T(8,128)(2,1)}), bf16[128,64,128]{0,2,1:T(8,128)(2,1)S(1)}, u32[]{:S(2)}, u32[]{:S(2)}) async-start(bf16[128,64,128]{0,2,1:T(8,128)(2,1)} %bitcast.13), calls=%async_computation | async-start | bytes 4194304 | tf_op jit(solution)/shard_map/all_to_all | solution.py:74
  26.2 180.8 %all-gather.3.cloned.1.call-start = ((), (), s32[]{:S(2)}) async-start(), calls=%async_computation.3 | async-start | bytes 8519680 | tf_op jit(solution)/shard_map/all_gather | solution.py:55
  106.7 9.3 %copy-start.5 = (f32[512]{0:T(512)S(1)}, f32[512]{0:T(512)}, u32[]{:S(2)}) copy-start(f32[512]{0:T(512)} %param.13) | copy-start | bytes 6148
  106.7 18.6 %copy-start.6 = (f32[512]{0:T(512)S(1)}, f32[512]{0:T(512)}, u32[]{:S(2)}) copy-start(f32[512]{0:T(512)} %param.14) | copy-start | bytes 6148
  106.7 100.3 %copy-start.2 = (bf16[128,512]{1,0:T(8,128)(2,1)S(1)}, bf16[128,512]{1,0:T(8,128)(2,1)}, u32[]{:S(2)}) copy-start(bf16[128,512]{1,0:T(8,128)(2,1)} %get-tuple-element.69) | copy-start | bytes 393220
  106.7 1.4 copy-start.1
  126.1 138.0 %reduce-scatter.2.cloned.1.call-start = ((), (), s32[]{:S(2)}) async-start(), calls=%async_computation.5 | async-start | bytes 5242880 | tf_op jit(solution)/shard_map/reduce_scatter | solution.py:73
  207.0 6.4 %copy-start = (bf16[8192,512]{1,0:T(8,128)(2,1)S(1)}, bf16[8192,512]{1,0:T(8,128)(2,1)}, u32[]{:S(2)}) copy-start(bf16[8192,512]{1,0:T(8,128)(2,1)} %get-tuple-element.29) | copy-start | bytes 25165828 | tf_op jit(solution)/shard_map/cond
  218.2 19.6 %copy-start.4 = (bf16[128,512]{1,0:T(8,128)(2,1)S(1)}, bf16[128,512]{1,0:T(8,128)(2,1)}, u32[]{:S(2)}) copy-start(bf16[128,512]{1,0:T(8,128)(2,1)} %param.17) | copy-start | bytes 393220
  218.2 19.6 %copy-start.7 = (f32[128]{0:T(128)S(1)}, f32[128]{0:T(128)}, u32[]{:S(2)}) copy-start(f32[128]{0:T(128)} %param.16) | copy-start | bytes 1540
Sparse Core Ops, SparseCore 0:
  11.3 95.2 all-gather.4
  126.2 80.7 all-gather.2
  218.4 45.6 reduce-scatter.1
where the time goes:
time: 271 us
  waiting for transfers between devices  178 us (66%)
  blocking collectives  36.8 us (14%)
  matrix products  15 us (6%)
  between operations  13.8 us (5%)
  starting transfers between devices  13.3 us (5%)
  local copies, waits for them, and re-layouts  10.4 us (4%)
  other arithmetic  3.82 us (1%)
    all_gather x1, waiting for transfers between devices, per_device(): shard_rows = lax.all_gather(normed, 'seq', axis=0, tiled=True)  80.8 us
    all_to_all x1, waiting for transfers between devices, per_device(): lax.all_to_all(token_weight, 'seq', split_axis=1, concat_axis=0, tiled=True)  48.1 us
    reduce_scatter x1, waiting for transfers between devices, per_device(): lax.psum_scatter(weight_term, 'hid', scatter_dimension=1, tiled=True)  25.5 us
    all_gather x1, waiting for transfers between devices, per_device(): fold_shard_rows = lax.all_gather(grad_mix, 'seq', axis=0, tiled=True)  23.1 us
    all_to_all x1, blocking collectives, sent_to_all(): return lax.all_to_all(copies, axis, split_axis=0, concat_axis=0, tiled=True)  18.7 us
    all_to_all x1, starting transfers between devices, per_device(): lax.all_to_all(token_weight, 'seq', split_axis=1, concat_axis=0, tiled=True)  13.1 us
    psum x1, blocking collectives, per_device(): lax.psum((jnp.sum(second, axis=1), jnp.sum(second * second, axis=1), jnp....  9.12 us
    psum x1, blocking collectives, per_device(): lax.psum((jnp.sum(grad_centred, axis=1), jnp.sum(grad_centred * centred,...  8.99 us
  transfers between devices with their start and end apart: 4, of which 4 were waited for; matrix products, arithmetic and copies ran while one was open for 2% of the time, Pallas kernels for 0%

commit v1 on v0

v1 whole, which is shorter than its diff:
```python
import functools

import jax
import jax.numpy as jnp
from jax import lax
from jax.experimental import pallas as pl
from jax.experimental.pallas import tpu as pltpu
from jax.sharding import PartitionSpec as P

MESH = pl.DeviceIdType.MESH
F32 = jnp.float32
BF16 = jnp.bfloat16
T = 128
R = 8
Z = 8
X = 4


def dot(a, b, ca, cb):
    return lax.dot_general(a, b, (((ca,), (cb,)), ((), ())), preferred_element_type=F32)


def kernel(
    hidden,
    gate, value, gain, shift, w, tbias, go,
    gg_out, gv_out, gs_out, gw_out, tb_out,
    g_all, n_all, wt, s_acc, s_send, s_recv, gn_own, gn_send, gn_recv, gw_send, gwx_recv, gwr, gwf,
    stat1, stat2, red1, red2, cen, rows,
    g_ss, g_rs, w_ss, w_rs, n_ss, n_rs, s_ss, s_rs, gn_ss, gn_rs, gx_ss, gx_rs, gf_ss, gf_rs,
    st_ss, st_rs, sp_ss, sp_rs, ra_ss, ra_rs, rb_ss, rb_rs,
):
    s = lax.axis_index("seq")
    x = lax.axis_index("hid")
    z = s // R
    r = s % R

    def rcopy(src, dst, ss, rs, ds, dx):
        return pltpu.make_async_remote_copy(
            src_ref=src, dst_ref=dst, send_sem=ss, recv_sem=rs,
            device_id=(ds, dx), device_id_type=MESH,
        )

    def plane(d):
        q = (r + d) % R
        return q, z * R + q

    barrier = pltpu.get_barrier_semaphore()
    for d in range(1, R):
        q, dev = plane(d)
        pl.semaphore_signal(barrier, inc=1, device_id=(dev, x), device_id_type=MESH)
    for d in range(1, Z):
        pl.semaphore_signal(
            barrier, inc=1, device_id=(((z + d) % Z) * R + r, x), device_id_type=MESH
        )
    for d in range(1, X):
        pl.semaphore_signal(barrier, inc=1, device_id=(s, (x + d) % X), device_id_type=MESH)

    v = value[...].astype(F32)
    gm = (go[...].astype(F32) * gate[...].astype(F32)).astype(BF16)
    g_all[r] = gm
    lane = lax.broadcasted_iota(jnp.int32, (T, T), 1)

    def as_rows(cols):
        m = jnp.zeros((T, T), F32)
        for i, col in enumerate(cols):
            m = jnp.where(lane == i, col, m)
        return m.T[:8]

    stat1[x] = as_rows((
        jnp.sum(v, axis=1, keepdims=True),
        jnp.sum(v * v, axis=1, keepdims=True),
        jnp.sum(gm.astype(F32), axis=1, keepdims=True),
    ))
    pl.semaphore_wait(barrier, (R - 1) + (Z - 1) + (X - 1))

    def x_send(buf, ss, rs):
        for d in range(1, X):
            t = (x + d) % X
            rcopy(buf.at[x], buf.at[x], ss.at[d], rs.at[x], s, t).start()

    def x_wait(buf, ss, rs):
        for d in range(1, X):
            t = (x + d) % X
            c = rcopy(buf.at[x], buf.at[t], ss.at[d], rs.at[t], s, t)
            c.wait_recv()
            c.wait_send()

    x_send(stat1, st_ss, st_rs)
    for d in range(1, R):
        q, dev = plane(d)
        rcopy(g_all.at[r], g_all.at[r], g_ss.at[d], g_rs.at[r], dev, x).start()

    def w_send(k, carry):
        zz = z - k
        for d in range(1, R):
            q, dev = plane(d)
            cols = pl.ds(pl.multiple_of((zz * R + q) * T, T), T)
            rcopy(w.at[:, cols], wt.at[zz, r], w_ss.at[zz, d], w_rs.at[zz, r], dev, x).start()
        return carry

    lax.fori_loop(0, z + 1, w_send, 0)

    x_wait(stat1, st_ss, st_rs)
    tot = stat1[0] + stat1[1] + stat1[2] + stat1[3]
    tb_out[...] = tot[2:3]
    colm = jnp.concatenate([tot[:3], tbias[...], jnp.zeros((T - 4, T), F32)], axis=0).T
    mean = colm[:, 0:1] / hidden
    var = colm[:, 1:2] / hidden - mean * mean
    inv = lax.rsqrt(var + 1e-05)
    centred = (v - mean) * inv
    cen[...] = centred
    rows[0] = jnp.broadcast_to(inv, (T, T))
    rows[1] = jnp.broadcast_to(colm[:, 3:4], (T, T))
    n_all[z] = (centred * gain[...] + shift[...]).astype(BF16)

    def n_send(k, carry):
        zz = Z - 1 - k
        rcopy(n_all.at[z], n_all.at[z], n_ss.at[zz], n_rs.at[z], zz * R + r, x).start()
        return carry

    lax.fori_loop(0, Z - 1 - z, n_send, 0)

    for d in range(1, R):
        q, dev = plane(d)
        rcopy(g_all.at[q], g_all.at[q], g_ss.at[d], g_rs.at[q], dev, x).wait_recv()

    def step(k, carry):
        zz = z - k
        for d in range(1, R):
            q, dev = plane(d)
            rcopy(wt.at[zz, q], wt.at[zz, q], w_ss.at[zz, d], w_rs.at[zz, q], dev, x).wait_recv()
        wt[zz, r] = w[:, pl.ds(pl.multiple_of((zz * R + r) * T, T), T)]

        @pl.when(k == 0)
        def _():
            row = lax.broadcasted_iota(jnp.int32, (T, T), 0)
            own = wt[zz, r].astype(F32)
            wt[zz, r] = jnp.where(row >= lane, own, 0.0).astype(BF16)

            def clear(q, c):
                wt[zz, q] = jnp.zeros((T, T), BF16)
                return c

            lax.fori_loop(0, r, clear, 0)

        wz = wt[zz].reshape(R * T, T)
        gz = g_all[...].reshape(R * T, -1)
        gn = dot(wz, gz, 0, 0)

        @pl.when(k == 0)
        def _():
            gn_own[...] = gn

        @pl.when(k > 0)
        def _():
            gn_send[zz] = gn.astype(BF16)
            rcopy(
                gn_send.at[zz], gn_recv.at[z], gn_ss.at[zz], gn_rs.at[z], zz * R + r, x
            ).start()
            rcopy(
                n_all.at[zz], n_all.at[zz], n_ss.at[zz], n_rs.at[zz], zz * R + r, x
            ).wait_recv()

        nz = n_all[zz]
        gw_send[zz] = dot(gz, nz, 1, 1).astype(BF16)
        t = zz // 2

        @pl.when(t != x)
        def _():
            rcopy(
                gw_send.at[zz], gwx_recv.at[zz % 2, x], gx_ss.at[zz], gx_rs.at[zz % 2, x], s, t
            ).start()

        sp = dot(wz, nz, 1, 0)

        @pl.when(k == 0)
        def _():
            s_acc[...] = sp

        @pl.when(k > 0)
        def _():
            s_acc[...] += sp

        return carry

    lax.fori_loop(0, z + 1, step, 0)

    for d in range(1, R):
        q, dev = plane(d)
        s_send[q] = s_acc[pl.ds(pl.multiple_of(q * T, T), T), :].astype(BF16)
        rcopy(s_send.at[q], s_recv.at[r], s_ss.at[d], s_rs.at[r], dev, x).start()

    for b in range(2):
        zb = 2 * x + b

        @pl.when(zb <= z)
        def _():
            acc = gw_send[zb].astype(F32)
            for d in range(1, X):
                t = (x + d) % X
                rcopy(
                    gw_send.at[zb], gwx_recv.at[b, t], gx_ss.at[zb], gx_rs.at[b, t], s, t
                ).wait_recv()
                acc = acc + gwx_recv[b, t].astype(F32)
            gwr[b] = acc.astype(BF16).reshape(R, T, T)
            for d in range(1, R):
                q, dev = plane(d)
                rcopy(
                    gwr.at[b, q], gwf.at[b, r], gf_ss.at[b, d], gf_rs.at[b, r], dev, x
                ).start()
            gwf[b, r] = gwr[b, r]

        @pl.when(zb > z)
        def _():
            gwf[b] = jnp.zeros((R, T, T), BF16)

    acc = s_acc[pl.ds(pl.multiple_of(r * T, T), T), :]
    for d in range(1, R):
        q, dev = plane(d)
        rcopy(s_send.at[q], s_recv.at[q], s_ss.at[d], s_rs.at[q], dev, x).wait_recv()
        acc = acc + s_recv[q].astype(F32)
    gg_out[...] = (go[...].astype(F32) * (acc + rows[1][:, 0:1])).astype(BF16)

    def gn_wait(k, carry):
        zz = z + 1 + k
        rcopy(
            gn_send.at[zz], gn_recv.at[zz], gn_ss.at[zz], gn_rs.at[zz], zz * R + r, x
        ).wait_recv()
        gn_own[...] += gn_recv[zz].astype(F32)
        return carry

    lax.fori_loop(0, Z - 1 - z, gn_wait, 0)
    gn = gn_own[...]
    centred = cen[...]
    gc = gn * gain[...]
    stat2[x] = as_rows((
        jnp.sum(gc, axis=1, keepdims=True),
        jnp.sum(gc * centred, axis=1, keepdims=True),
    ))
    x_send(stat2, sp_ss, sp_rs)
    red1[r] = jnp.concatenate([
        jnp.sum(gn * centred, axis=0, keepdims=True),
        jnp.sum(gn, axis=0, keepdims=True),
        jnp.zeros((6, gn.shape[1]), F32),
    ], axis=0)
    for d in range(1, R):
        q, dev = plane(d)
        rcopy(red1.at[r], red1.at[r], ra_ss.at[d], ra_rs.at[r], dev, x).start()
    x_wait(stat2, sp_ss, sp_rs)
    tot = stat2[0] + stat2[1] + stat2[2] + stat2[3]
    colm = jnp.concatenate([tot, jnp.zeros((T - 8, T), F32)], axis=0).T
    gv_out[...] = (
        rows[0][:, 0:1] * (gc - colm[:, 0:1] / hidden - centred * (colm[:, 1:2] / hidden))
    ).astype(BF16)
    for d in range(1, R):
        q, dev = plane(d)
        c = rcopy(red1.at[r], red1.at[q], ra_ss.at[d], ra_rs.at[q], dev, x)
        c.wait_recv()
        c.wait_send()
    tot = red1[0]
    for q in range(1, R):
        tot = tot + red1[q]
    red2[z] = tot
    for d in range(1, Z):
        zz = (z + d) % Z
        rcopy(red2.at[z], red2.at[z], rb_ss.at[d], rb_rs.at[z], zz * R + r, x).start()

    for b in range(2):
        zb = 2 * x + b

        @pl.when(zb <= z)
        def _():
            for d in range(1, R):
                q, dev = plane(d)
                c = rcopy(gwr.at[b, q], gwf.at[b, q], gf_ss.at[b, d], gf_rs.at[b, q], dev, x)
                c.wait_recv()
                c.wait_send()

        for q in range(R):
            gw_out[:, (b * R + q) * T : (b * R + q + 1) * T] = gwf[b, q]

    for d in range(1, Z):
        zz = (z + d) % Z
        c = rcopy(red2.at[z], red2.at[zz], rb_ss.at[d], rb_rs.at[zz], zz * R + r, x)
        c.wait_recv()
        c.wait_send()
    tot = red2[0]
    for q in range(1, Z):
        tot = tot + red2[q]
    gs_out[...] = tot

    for d in range(1, R):
        q, dev = plane(d)
        rcopy(g_all.at[r], g_all.at[r], g_ss.at[d], g_rs.at[r], dev, x).wait_send()
        rcopy(s_send.at[q], s_recv.at[r], s_ss.at[d], s_rs.at[r], dev, x).wait_send()

    def drain_w(zz, carry):
        for d in range(1, R):
            q, dev = plane(d)
            rcopy(wt.at[zz, q], wt.at[zz, r], w_ss.at[zz, d], w_rs.at[zz, r], dev, x).wait_send()

        @pl.when(zz // 2 != x)
        def _():
            rcopy(
                gw_send.at[zz], gwx_recv.at[zz % 2, x], gx_ss.at[zz], gx_rs.at[zz % 2, x],
                s, zz // 2,
            ).wait_send()

        return carry

    lax.fori_loop(0, z + 1, drain_w, 0)

    def drain_gn(zz, carry):
        rcopy(
            gn_send.at[zz], gn_recv.at[z], gn_ss.at[zz], gn_rs.at[z], zz * R + r, x
        ).wait_send()
        return carry

    lax.fori_loop(0, z, drain_gn, 0)

    def drain_n(zz, carry):
        rcopy(n_all.at[z], n_all.at[z], n_ss.at[zz], n_rs.at[z], zz * R + r, x).wait_send()
        return carry

    lax.fori_loop(z + 1, Z, drain_n, 0)


def per_device(gate_half, value_half, norm_gain, norm_shift, token_weight, token_bias, grad_output):
    rows, chans = gate_half.shape
    cols = token_weight.shape[1]
    width = cols // X
    dma = pltpu.SemaphoreType.DMA
    vmem = pl.BlockSpec(memory_space=pltpu.VMEM)
    gg, gv, gs, gw, tb = pl.pallas_call(
        functools.partial(kernel, chans * X),
        out_shape=(
            jax.ShapeDtypeStruct((rows, chans), BF16),
            jax.ShapeDtypeStruct((rows, chans), BF16),
            jax.ShapeDtypeStruct((8, chans), F32),
            jax.ShapeDtypeStruct((rows, width), BF16),
            jax.ShapeDtypeStruct((1, rows), F32),
        ),
        in_specs=[vmem] * 7,
        out_specs=(vmem,) * 5,
        scratch_shapes=[
            pltpu.VMEM((R, T, chans), BF16),
            pltpu.VMEM((Z, T, chans), BF16),
            pltpu.VMEM((Z, R, T, T), BF16),
            pltpu.VMEM((R * T, chans), F32),
            pltpu.VMEM((R, T, chans), BF16),
            pltpu.VMEM((R, T, chans), BF16),
            pltpu.VMEM((T, chans), F32),
            pltpu.VMEM((Z, T, chans), BF16),
            pltpu.VMEM((Z, T, chans), BF16),
            pltpu.VMEM((Z, R * T, T), BF16),
            pltpu.VMEM((2, X, R * T, T), BF16),
            pltpu.VMEM((2, R, T, T), BF16),
            pltpu.VMEM((2, R, T, T), BF16),
            pltpu.VMEM((X, 8, T), F32),
            pltpu.VMEM((X, 8, T), F32),
            pltpu.VMEM((R, 8, chans), F32),
            pltpu.VMEM((Z, 8, chans), F32),
            pltpu.VMEM((T, chans), F32),
            pltpu.VMEM((2, T, T), F32),
            dma((R,)), dma((R,)),
            dma((Z, R)), dma((Z, R)),
            dma((Z,)), dma((Z,)),
            dma((R,)), dma((R,)),
            dma((Z,)), dma((Z,)),
            dma((Z,)), dma((2, X)),
            dma((2, R)), dma((2, R)),
            dma((X,)), dma((X,)),
            dma((X,)), dma((X,)),
            dma((R,)), dma((R,)),
            dma((Z,)), dma((Z,)),
        ],
        compiler_params=pltpu.CompilerParams(
            collective_id=0, has_side_effects=True, vmem_limit_bytes=48 * 1024 * 1024
        ),
    )(
        gate_half, value_half, norm_gain[None], norm_shift[None], token_weight, token_bias[None],
        grad_output,
    )
    row = lax.axis_index("seq") * rows + lax.iota(jnp.int32, rows)[:, None]
    col = lax.axis_index("hid") * width + lax.iota(jnp.int32, width)[None, :]
    grad_weight = jnp.where(col <= row, gw.astype(F32), 0.0)
    return gg, gv, gs[0], gs[1], grad_weight, tb[0]


def solution(mesh):
    placed = (
        P("seq", "hid"),
        P("seq", "hid"),
        P("hid"),
        P("hid"),
        P("seq", None),
        P("seq"),
        P("seq", "hid"),
    )
    return jax.shard_map(
        per_device,
        mesh=mesh,
        in_specs=placed,
        out_specs=(P("seq", "hid"), P("seq", "hid"), P("hid"), P("hid"), P("seq", "hid"), P("seq")),
        check_vma=False,
    )
```

time: 271 us -> 95.6 us (0.35)
  waiting for transfers between devices: 178 us -> 0 us
  Pallas kernels: 0 us -> 84.8 us
  blocking collectives: 36.8 us -> 0 us
  matrix products: 15 us -> 0 us
  starting transfers between devices: 13.3 us -> 0 us
  between operations: 13.8 us -> 0.68 us
    all_gather x2 -> x0, waiting for transfers between devices: 104 us -> none  [the longest x1 80.8 us: per_device(): shard_rows = lax.all_gather(normed, 'seq', axis=0, tiled=True)]
    pallas_call x0 -> x1, Pallas kernels: none -> 84.8 us  [per_device(): pl.pallas_call(functools.partial(kernel, chans * X), out_shape=(jax.Shape...]
    all_to_all x1 -> x0, waiting for transfers between devices: 48.1 us -> none  [per_device(): lax.all_to_all(token_weight, 'seq', split_axis=1, concat_axis=0, tiled=True)]
    reduce_scatter x1 -> x0, waiting for transfers between devices: 25.5 us -> none  [per_device(): lax.psum_scatter(weight_term, 'hid', scatter_dimension=1, tiled=True)]
    all_to_all x1 -> x0, blocking collectives: 18.7 us -> none  [sent_to_all(): return lax.all_to_all(copies, axis, split_axis=0, concat_axis=0, tiled=True)]
    psum x2 -> x0, blocking collectives: 18.1 us -> none  [the longest x1 9.12 us: per_device(): lax.psum((jnp.sum(second, axis=1), jnp.sum(second * second, axis=1), jnp....]
    dot_general x3 -> x0, matrix products: 15 us -> none  [the longest x1 5.45 us: compute(): jnp.dot(weight_block, shard_rows, preferred_element_type=jnp.float32)]
    all_to_all x1 -> x0, starting transfers between devices: 13.1 us -> none  [per_device(): lax.all_to_all(token_weight, 'seq', split_axis=1, concat_axis=0, tiled=True)]
  transfers between devices with their start and end apart: 4 -> 0, of which waited for: 4 -> 0; matrix products, arithmetic and copies ran while one was open for 2% -> 0% of each run, Pallas kernels for 0% -> 0%
where the time goes in v1:
time: 95.6 us; the launch traced here: 95.4 us
  Pallas kernels  84.8 us (89%)
  local copies, waits for them, and re-layouts  8.72 us (9%)
  other arithmetic  1.15 us (1%)
    pallas_call x1, Pallas kernels, per_device(): pl.pallas_call(functools.partial(kernel, chans * X), out_shape=(jax.Shape...  84.8 us
    unnamed x17, local copies, waits for them, and re-layouts  8.13 us

profile of v1, /device:TPU:1, one launch (start us, length us, event | category | flops | bytes accessed | tf_op | source)
XLA Modules:
  0.0 95.4 jit_solution(1345800606589865503)
XLA Ops:
  0.7 0.0 copy-start
  0.7 1.6 %copy-done = bf16[128,8192]{1,0:T(8,128)(2,1)S(1)} copy-done((bf16[128,8192]{1,0:T(8,128)(2,1)S(1)}, bf16[128,8192]{1,0:T(8,128)(2,1)}, u32[]{:S(2)}) %copy-start) | copy-done | bytes 2097176
  2.3 0.0 copy-start.1
  2.3 0.9 copy-done.1
  3.2 0.0 copy-start.2
  3.2 0.9 copy-done.2
  4.1 0.0 copy-start.3
  4.1 0.9 copy-done.3
  5.0 0.0 copy-start.4
  5.0 0.7 copy-done.4
  5.7 0.0 copy-start.5
  5.7 0.7 copy-done.5
  6.3 0.0 copy-start.6
  6.3 0.7 copy-done.6
  7.0 84.8 %shard_map.118 = (bf16[128,512]{1,0:T(8,128)(2,1)S(1)}, bf16[128,512]{1,0:T(8,128)(2,1)S(1)}, f32[8,512]{1,0:T(8,128)S(1)}, bf16[128,2048]{1,0:T(8,128)(2,1)S(1)}, f32[1,128]{1,0:T(1,128)S(1)}) custom-call(bf16[128,512]{1,0:T(8,128)(2,1)S(1)} %copy-done.1, bf16[128,512]{1,0:T(8,128)(2,1)S(1)} %copy-done.2, f32[1,512]{1,0:T(1,128)S(1)} %bitcast.6, ...), custom_call_target="tpu_custom_call" | custom-call | tf_op jit(solution)/shard_map/pallas_call | solution.py:334
  91.8 0.6 fusion
  92.4 1.1 %convert_select_fusion = f32[128,2048]{1,0:T(8,128)} fusion(bf16[128,2048]{1,0:T(8,128)(2,1)S(1)} %get-tuple-element.14, s32[2048]{0:T(1024)S(1)} %iota_add_fusion, s32[128]{0:T(128)S(1)} %iota_add_fusion.1), kind=kLoop, calls=%fused_computation | loop fusion | flops 786432 | bytes 1581568 | tf_op jit(solution)/shard_map/jit(_where)/select_n | solution.py:386
  93.5 0.7 copy.16
  94.2 0.7 copy.17
  94.9 0.5 copy.18
  (2 shorter events, 0.0 us)
Async XLA Ops:
  0.7 1.6 %copy-start = (bf16[128,8192]{1,0:T(8,128)(2,1)S(1)}, bf16[128,8192]{1,0:T(8,128)(2,1)}, u32[]{:S(2)}) copy-start(bf16[128,8192]{1,0:T(8,128)(2,1)} %w.1) | copy-start | bytes 6291460
  2.3 0.9 copy-start.1
  3.2 0.9 copy-start.2
  4.1 0.9 copy-start.3
  5.0 0.7 copy-start.4
  5.7 0.7 copy-start.5
  6.3 0.7 copy-start.6

commit v2 on v1

v2 whole, which is shorter than its diff:
```python
import contextlib
import functools

import jax
import jax.numpy as jnp
from jax import lax
from jax.experimental import pallas as pl
from jax.experimental.pallas import tpu as pltpu
from jax.sharding import PartitionSpec as P

MESH = pl.DeviceIdType.MESH
F32 = jnp.float32
BF16 = jnp.bfloat16
T = 128
R = 8
Z = 8
X = 4
Y = 4


def at(name):
    return contextlib.nullcontext()


def dot(a, b, ca, cb):
    return lax.dot_general(a, b, (((ca,), (cb,)), ((), ())), preferred_element_type=F32)


def kernel(
    hidden,
    gate_h, value_h, gain_h, shift_h, w_h, tbias_h, go_h,
    gg_out, gv_out, gs_out, gw_out, tb_out,
    g_all, n_all, wt, s_acc, s_sib, s_send, s_recv, gn_own, gn_send, gn_recv,
    gw_send, gwo, gwx, gwr, gwf,
    stat1, stat2, red1, red2, cen, rows,
    gate, value, gain, shift, w, tbias, go, in_sem,
    gg, gv, gs, gw, tb, out_sem,
    g_ss, g_rs, w_ss, w_rs, n_ss, n_rs, sb_ss, sb_rs, s_ss, s_rs, gn_ss, gn_rs,
    go_ss, go_rs, gx_ss, gx_rs, gf_ss, gf_rs,
    st_ss, st_rs, sp_ss, sp_rs, ra_ss, ra_rs, rb_ss, rb_rs,
):
    s = lax.axis_index("seq")
    x = lax.axis_index("hid")
    z = s // R
    r = s % R
    y = r // 2
    c = r % 2
    sib = z * R + y * 2 + (1 - c)
    H = R * T // 2

    def rcopy(src, dst, ss, rs, ds, dx):
        return pltpu.make_async_remote_copy(
            src_ref=src, dst_ref=dst, send_sem=ss, recv_sem=rs,
            device_id=(ds, dx), device_id_type=MESH,
        )

    def plane(d):
        q = (r + d) % R
        return q, z * R + q

    def across(e):
        q = (y + e) % Y * 2 + c
        return q, z * R + q

    def chunk(k, core):
        k = (k + core * ((z + 1) // 2)) % (z + 1)
        evens = (z + 2) // 2
        return jnp.where(k < evens, 2 * k, 2 * (k - evens) + 1)

    loads = [
        pltpu.make_async_copy(a, b, in_sem.at[i])
        for i, (a, b) in enumerate((
            (value_h, value), (go_h, go), (gate_h, gate), (w_h, w),
            (gain_h, gain), (shift_h, shift), (tbias_h, tbias),
        ))
    ]
    for load in loads:
        load.start()

    barrier = pltpu.get_barrier_semaphore()
    for d in range(1, R):
        q, dev = plane(d)
        pl.semaphore_signal(barrier, inc=1, device_id=(dev, x), device_id_type=MESH)
    for d in range(1, Z):
        pl.semaphore_signal(
            barrier, inc=1, device_id=((z + d) % Z * R + r, x), device_id_type=MESH
        )
    for d in range(1, X):
        pl.semaphore_signal(barrier, inc=1, device_id=(s, (x + d) % X), device_id_type=MESH)

    for load in loads[:3]:
        load.wait()
    v = value[...].astype(F32)
    gm = (go[...].astype(F32) * gate[...].astype(F32)).astype(BF16)
    g_all[r] = gm
    lane = lax.broadcasted_iota(jnp.int32, (T, T), 1)

    def as_rows(cols):
        m = jnp.zeros((T, T), F32)
        for i, col in enumerate(cols):
            m = jnp.where(lane == i, col, m)
        return m.T[:8]

    stat1[x] = as_rows((
        jnp.sum(v, axis=1, keepdims=True),
        jnp.sum(v * v, axis=1, keepdims=True),
        jnp.sum(gm.astype(F32), axis=1, keepdims=True),
    ))
    for load in loads[3:]:
        load.wait()
    with at("barrier"):
        pl.semaphore_wait(barrier, (R - 1) + (Z - 1) + (X - 1))

    def x_send(buf, ss, rs):
        for d in range(1, X):
            t = (x + d) % X
            rcopy(buf.at[x], buf.at[x], ss.at[d], rs.at[x], s, t).start()

    def x_wait(buf, ss, rs):
        for d in range(1, X):
            t = (x + d) % X
            cp = rcopy(buf.at[x], buf.at[t], ss.at[d], rs.at[t], s, t)
            cp.wait_recv()
            cp.wait_send()

    x_send(stat1, st_ss, st_rs)
    for e in (1, 3, 2):
        q, dev = across(e)
        rcopy(g_all.at[r], g_all.at[r], g_ss.at[e], g_rs.at[r], dev, x).start()
    rcopy(g_all.at[r], g_all.at[r], g_ss.at[4], g_rs.at[r], sib, x).start()

    def w_send(k, carry):
        for d in range(1, R):
            q, dev = plane(d)
            zz = chunk(k, q % 2)
            cols = pl.ds(pl.multiple_of((zz * R + q) * T, T), T)
            rcopy(w.at[:, cols], wt.at[zz, r], w_ss.at[zz, d], w_rs.at[zz, r], dev, x).start()
        return carry

    with at("w send"):
        lax.fori_loop(0, z + 1, w_send, 0)

    with at("stat wait"):
        x_wait(stat1, st_ss, st_rs)
    tot = stat1[0] + stat1[1] + stat1[2] + stat1[3]
    tb[...] = tot[2:3]
    colm = jnp.concatenate([tot[:3], tbias[...], jnp.zeros((T - 4, T), F32)], axis=0).T
    mean = colm[:, 0:1] / hidden
    var = colm[:, 1:2] / hidden - mean * mean
    inv = lax.rsqrt(var + 1e-05)
    centred = (v - mean) * inv
    cen[...] = centred
    rows[0] = jnp.broadcast_to(inv, (T, T))
    rows[1] = jnp.broadcast_to(colm[:, 3:4], (T, T))
    n_all[z] = (centred * gain[...] + shift[...]).astype(BF16)

    def n_send(k, carry):
        zz = Z - 1 - k
        rcopy(n_all.at[z], n_all.at[z], n_ss.at[zz], n_rs.at[z], zz * R + r, x).start()
        return carry

    with at("n send"):
        lax.fori_loop(0, Z - 1 - z, n_send, 0)

    with at("g wait"):
        for e in (1, 3, 2):
            q, dev = across(e)
            rcopy(g_all.at[q], g_all.at[q], g_ss.at[e], g_rs.at[q], dev, x).wait_recv()
            rcopy(g_all.at[q], g_all.at[q], g_ss.at[4 + e], g_rs.at[q], sib, x).start()
        for e in range(Y):
            q = (y + e) % Y * 2 + (1 - c)
            rcopy(g_all.at[q], g_all.at[q], g_ss.at[4], g_rs.at[q], sib, x).wait_recv()

    def grad_part(k):
        zz = chunk(k, c)
        with at("w wait"):
            for d in range(1, R):
                q, dev = plane(d)
                rcopy(wt.at[zz, q], wt.at[zz, q], w_ss.at[zz, d], w_rs.at[zz, q], dev, x).wait_recv()
        wt[zz, r] = w[:, pl.ds(pl.multiple_of((zz * R + r) * T, T), T)]

        @pl.when(zz == z)
        def _():
            row = lax.broadcasted_iota(jnp.int32, (T, T), 0)
            own = wt[zz, r].astype(F32)
            wt[zz, r] = jnp.where(row >= lane, own, 0.0).astype(BF16)

            def clear(q, carry):
                wt[zz, q] = jnp.zeros((T, T), BF16)
                return carry

            lax.fori_loop(0, r, clear, 0)

        gn = dot(wt[zz].reshape(R * T, T), g_all[...].reshape(R * T, -1), 0, 0)

        @pl.when(zz == z)
        def _():
            gn_own[...] = gn

        @pl.when(zz != z)
        def _():
            gn_send[zz] = gn.astype(BF16)
            rcopy(
                gn_send.at[zz], gn_recv.at[z], gn_ss.at[zz], gn_rs.at[z], zz * R + r, x
            ).start()

    def half(ref, h):
        return ref.at[pl.ds(pl.multiple_of(h * H, H), H), :]

    def norm_part(j):
        zz = chunk(j, c)

        @pl.when(zz != z)
        def _():
            with at("n wait"):
                rcopy(
                    n_all.at[zz], n_all.at[zz], n_ss.at[zz], n_rs.at[zz], zz * R + r, x
                ).wait_recv()

        nz = n_all[zz]
        gw_send[zz] = dot(g_all[...].reshape(R * T, -1), nz, 1, 1).astype(BF16)
        t = zz // 2
        role = (x - t + X) % X

        @pl.when(role == 2)
        def _():
            for h, e in ((0, 1), (1, 3)):
                rcopy(
                    half(gw_send.at[zz], h), gwo.at[zz], go_ss.at[zz, h], go_rs.at[zz],
                    s, (t + e) % X,
                ).start()

        @pl.when(role % 2 == 1)
        def _():
            side = role // 2
            h = 1 - side
            rcopy(
                half(gw_send.at[zz], h), half(gwx.at[zz % 2, side], h),
                gx_ss.at[zz, h], gx_rs.at[zz % 2, side, h], s, t,
            ).start()

        sp = dot(wt[zz].reshape(R * T, T), nz, 1, 0).reshape(R, T, -1)

        @pl.when(j == 0)
        def _():
            s_acc[...] = sp

        @pl.when(j > 0)
        def _():
            s_acc[...] += sp

    def pass_part(j):
        zz = chunk(j, c)
        t = zz // 2
        role = (x - t + X) % X

        @pl.when(role % 2 == 1)
        def _():
            side = role // 2
            with at("gwo wait"):
                rcopy(gwo.at[zz], gwo.at[zz], go_ss.at[zz, 0], go_rs.at[zz], s, t).wait_recv()
            mine = half(gw_send.at[zz], side)
            mine[...] = (mine[...].astype(F32) + gwo[zz].astype(F32)).astype(BF16)
            rcopy(
                mine, half(gwx.at[zz % 2, side], side),
                gx_ss.at[zz, side], gx_rs.at[zz % 2, side, side], s, t,
            ).start()

    lag = jnp.where(z >= 5, 1, z + 1)

    def step(k, carry):
        @pl.when(k <= z)
        def _():
            grad_part(k)

        @pl.when((k >= lag) & (k <= z + lag))
        def _():
            norm_part(k - lag)

        @pl.when(k >= lag + 1)
        def _():
            pass_part(k - lag - 1)

        return carry

    lax.fori_loop(0, z + lag + 2, step, 0)

    for e in range(Y):
        q = (y + e) % Y
        rcopy(s_acc.at[q * 2 + 1 - c], s_sib.at[q], sb_ss.at[q], sb_rs.at[q], sib, x).start()
    with at("sib wait"):
        for e in (1, 3, 2, 0):
            q, dev = across(e)
            p = (y + e) % Y
            rcopy(s_acc.at[q], s_sib.at[p], sb_ss.at[p], sb_rs.at[p], sib, x).wait_recv()
            if e:
                s_send[p] = (s_acc[q] + s_sib[p]).astype(BF16)
                rcopy(s_send.at[p], s_recv.at[y], s_ss.at[e], s_rs.at[y], dev, x).start()

    for b in range(2):
        zb = 2 * x + b

        @pl.when(zb <= z)
        def _():
            with at("gwx wait"):
                for side in range(2):
                    for h in range(2):
                        rcopy(
                            half(gw_send.at[zb], h), half(gwx.at[b, side], h),
                            gx_ss.at[zb, h], gx_rs.at[b, side, h], s, (x + 1 + 2 * side) % X,
                        ).wait_recv()
            gwr[b] = (
                gw_send[zb].astype(F32) + gwx[b, 0].astype(F32) + gwx[b, 1].astype(F32)
            ).astype(BF16).reshape(R, T, T)
            for d in range(1, R):
                q, dev = plane(d)
                rcopy(
                    gwr.at[b, q], gwf.at[b, r], gf_ss.at[b, d], gf_rs.at[b, r], dev, x
                ).start()
            gwf[b, r] = gwr[b, r]

        @pl.when(zb > z)
        def _():
            gwf[b] = jnp.zeros((R, T, T), BF16)

    acc = s_acc[r] + s_sib[y]
    with at("s wait"):
        for e in (1, 3, 2):
            p = (y + e) % Y
            q, dev = across(e)
            rcopy(s_send.at[p], s_recv.at[p], s_ss.at[e], s_rs.at[p], dev, x).wait_recv()
            acc = acc + s_recv[p].astype(F32)
    gg[...] = (go[...].astype(F32) * (acc + rows[1][:, 0:1])).astype(BF16)
    stores = [
        pltpu.make_async_copy(a, b, out_sem.at[i])
        for i, (a, b) in enumerate(
            ((gg, gg_out), (tb, tb_out), (gv, gv_out), (gw, gw_out), (gs, gs_out))
        )
    ]
    stores[0].start()
    stores[1].start()

    def gn_wait(k, carry):
        zz = z + 1 + k
        rcopy(
            gn_send.at[zz], gn_recv.at[zz], gn_ss.at[zz], gn_rs.at[zz], zz * R + r, x
        ).wait_recv()
        gn_own[...] += gn_recv[zz].astype(F32)
        return carry

    with at("gn wait"):
        lax.fori_loop(0, Z - 1 - z, gn_wait, 0)
    gn = gn_own[...]
    centred = cen[...]
    gc = gn * gain[...]
    stat2[x] = as_rows((
        jnp.sum(gc, axis=1, keepdims=True),
        jnp.sum(gc * centred, axis=1, keepdims=True),
    ))
    x_send(stat2, sp_ss, sp_rs)
    red1[r] = jnp.concatenate([
        jnp.sum(gn * centred, axis=0, keepdims=True),
        jnp.sum(gn, axis=0, keepdims=True),
        jnp.zeros((6, gn.shape[1]), F32),
    ], axis=0)
    for d in range(1, R):
        q, dev = plane(d)
        rcopy(red1.at[r], red1.at[r], ra_ss.at[d], ra_rs.at[r], dev, x).start()
    with at("red1 wait"):
        for d in range(1, R):
            q, dev = plane(d)
            cp = rcopy(red1.at[r], red1.at[q], ra_ss.at[d], ra_rs.at[q], dev, x)
            cp.wait_recv()
            cp.wait_send()
    tot = red1[0]
    for q in range(1, R):
        tot = tot + red1[q]
    red2[z] = tot
    for d in range(1, Z):
        zz = (z + d) % Z
        rcopy(red2.at[z], red2.at[z], rb_ss.at[d], rb_rs.at[z], zz * R + r, x).start()
    with at("stat2 wait"):
        x_wait(stat2, sp_ss, sp_rs)
    tot = stat2[0] + stat2[1] + stat2[2] + stat2[3]
    colm = jnp.concatenate([tot, jnp.zeros((T - 8, T), F32)], axis=0).T
    gv[...] = (
        rows[0][:, 0:1] * (gc - colm[:, 0:1] / hidden - centred * (colm[:, 1:2] / hidden))
    ).astype(BF16)
    stores[2].start()

    for b in range(2):
        zb = 2 * x + b

        @pl.when(zb <= z)
        def _():
            with at("gwf wait"):
                for d in range(1, R):
                    q, dev = plane(d)
                    cp = rcopy(gwr.at[b, q], gwf.at[b, q], gf_ss.at[b, d], gf_rs.at[b, q], dev, x)
                    cp.wait_recv()
                    cp.wait_send()

        for q in range(R):
            gw[:, (b * R + q) * T : (b * R + q + 1) * T] = gwf[b, q]
    stores[3].start()

    for e in range(1, Y):
        q, dev = across(e)
        rcopy(g_all.at[r], g_all.at[r], g_ss.at[e], g_rs.at[r], dev, x).wait_send()
        rcopy(g_all.at[r], g_all.at[r], g_ss.at[4 + e], g_rs.at[r], sib, x).wait_send()
        p = (y + e) % Y
        rcopy(s_send.at[p], s_recv.at[y], s_ss.at[e], s_rs.at[y], dev, x).wait_send()
    rcopy(g_all.at[r], g_all.at[r], g_ss.at[4], g_rs.at[r], sib, x).wait_send()
    for q in range(Y):
        rcopy(s_acc.at[q * 2 + 1 - c], s_sib.at[q], sb_ss.at[q], sb_rs.at[q], sib, x).wait_send()

    def drain_w(zz, carry):
        for d in range(1, R):
            q, dev = plane(d)
            rcopy(wt.at[zz, q], wt.at[zz, r], w_ss.at[zz, d], w_rs.at[zz, r], dev, x).wait_send()
        role = (x - zz // 2 + X) % X

        @pl.when(role == 2)
        def _():
            for h in range(2):
                rcopy(
                    half(gw_send.at[zz], h), gwo.at[zz], go_ss.at[zz, h], go_rs.at[zz], s,
                    (x + 1) % X,
                ).wait_send()

        @pl.when(role % 2 == 1)
        def _():
            for h in range(2):
                rcopy(
                    half(gw_send.at[zz], h), half(gwx.at[0, 0], h),
                    gx_ss.at[zz, h], gx_rs.at[0, 0, h], s, (x + 1) % X,
                ).wait_send()

        return carry

    lax.fori_loop(0, z + 1, drain_w, 0)

    def drain_gn(zz, carry):
        rcopy(
            gn_send.at[zz], gn_recv.at[z], gn_ss.at[zz], gn_rs.at[z], zz * R + r, x
        ).wait_send()
        return carry

    lax.fori_loop(0, z, drain_gn, 0)

    def drain_n(zz, carry):
        rcopy(n_all.at[z], n_all.at[z], n_ss.at[zz], n_rs.at[z], zz * R + r, x).wait_send()
        return carry

    lax.fori_loop(z + 1, Z, drain_n, 0)

    with at("red2 wait"):
        for d in range(1, Z):
            zz = (z + d) % Z
            cp = rcopy(red2.at[z], red2.at[zz], rb_ss.at[d], rb_rs.at[zz], zz * R + r, x)
            cp.wait_recv()
            cp.wait_send()
    tot = red2[0]
    for q in range(1, Z):
        tot = tot + red2[q]
    gs[...] = tot
    stores[4].start()
    for store in stores:
        store.wait()


def per_device(gate_half, value_half, norm_gain, norm_shift, token_weight, token_bias, grad_output):
    rows, chans = gate_half.shape
    cols = token_weight.shape[1]
    width = cols // X
    dma = pltpu.SemaphoreType.DMA
    gg, gv, gs, gw, tb = pl.pallas_call(
        functools.partial(kernel, chans * X),
        out_shape=(
            jax.ShapeDtypeStruct((rows, chans), BF16),
            jax.ShapeDtypeStruct((rows, chans), BF16),
            jax.ShapeDtypeStruct((8, chans), F32),
            jax.ShapeDtypeStruct((rows, width), BF16),
            jax.ShapeDtypeStruct((1, rows), F32),
        ),
        in_specs=[pl.BlockSpec(memory_space=pl.ANY)] * 7,
        out_specs=(pl.BlockSpec(memory_space=pl.ANY),) * 5,
        scratch_shapes=[
            pltpu.VMEM((R, T, chans), BF16),
            pltpu.VMEM((Z, T, chans), BF16),
            pltpu.VMEM((Z, R, T, T), BF16),
            pltpu.VMEM((R, T, chans), F32),
            pltpu.VMEM((Y, T, chans), F32),
            pltpu.VMEM((Y, T, chans), BF16),
            pltpu.VMEM((Y, T, chans), BF16),
            pltpu.VMEM((T, chans), F32),
            pltpu.VMEM((Z, T, chans), BF16),
            pltpu.VMEM((Z, T, chans), BF16),
            pltpu.VMEM((Z, R * T, T), BF16),
            pltpu.VMEM((Z, R * T // 2, T), BF16),
            pltpu.VMEM((2, 2, R * T, T), BF16),
            pltpu.VMEM((2, R, T, T), BF16),
            pltpu.VMEM((2, R, T, T), BF16),
            pltpu.VMEM((X, 8, T), F32),
            pltpu.VMEM((X, 8, T), F32),
            pltpu.VMEM((R, 8, chans), F32),
            pltpu.VMEM((Z, 8, chans), F32),
            pltpu.VMEM((T, chans), F32),
            pltpu.VMEM((2, T, T), F32),
            pltpu.VMEM((rows, chans), BF16),
            pltpu.VMEM((rows, chans), BF16),
            pltpu.VMEM((1, chans), F32),
            pltpu.VMEM((1, chans), F32),
            pltpu.VMEM((rows, cols), BF16),
            pltpu.VMEM((1, rows), F32),
            pltpu.VMEM((rows, chans), BF16),
            dma((7,)),
            pltpu.VMEM((rows, chans), BF16),
            pltpu.VMEM((rows, chans), BF16),
            pltpu.VMEM((8, chans), F32),
            pltpu.VMEM((rows, width), BF16),
            pltpu.VMEM((1, rows), F32),
            dma((5,)),
            dma((R,)), dma((R,)),
            dma((Z, R)), dma((Z, R)),
            dma((Z,)), dma((Z,)),
            dma((Y,)), dma((Y,)),
            dma((Y,)), dma((Y,)),
            dma((Z,)), dma((Z,)),
            dma((Z, 2)), dma((Z,)),
            dma((Z, 2)), dma((2, 2, 2)),
            dma((2, R)), dma((2, R)),
            dma((X,)), dma((X,)),
            dma((X,)), dma((X,)),
            dma((R,)), dma((R,)),
            dma((Z,)), dma((Z,)),
        ],
        compiler_params=pltpu.CompilerParams(
            collective_id=0, has_side_effects=True, vmem_limit_bytes=60 * 1024 * 1024
        ),
    )(
        gate_half, value_half, norm_gain[None], norm_shift[None], token_weight, token_bias[None],
        grad_output,
    )
    row = lax.axis_index("seq") * rows + lax.iota(jnp.int32, rows)[:, None]
    col = lax.axis_index("hid") * width + lax.iota(jnp.int32, width)[None, :]
    grad_weight = jnp.where(col <= row, gw.astype(F32), 0.0)
    return gg, gv, gs[0], gs[1], grad_weight, tb[0]


def solution(mesh):
    placed = (
        P("seq", "hid"),
        P("seq", "hid"),
        P("hid"),
        P("hid"),
        P("seq", None),
        P("seq"),
        P("seq", "hid"),
    )
    return jax.shard_map(
        per_device,
        mesh=mesh,
        in_specs=placed,
        out_specs=(P("seq", "hid"), P("seq", "hid"), P("hid"), P("hid"), P("seq", "hid"), P("seq")),
        check_vma=False,
    )
```

time: 95.6 us -> 87.2 us (0.912)
  Pallas kernels: 84.8 us -> 78.5 us
  local copies, waits for them, and re-layouts: 8.72 us -> 5.03 us
  other arithmetic: 1.15 us -> 2.19 us
    pallas_call x1, Pallas kernels: 84.8 us -> 78.5 us  [per_device(): pl.pallas_call(functools.partial(kernel, chans * X), out_shape=(jax.Shape...]
    unnamed x17 -> x5, local copies, waits for them, and re-layouts: 8.13 us -> 3.65 us
    select_n x1, other arithmetic: 1.14 us -> 2.18 us  [per_device(): grad_weight = jnp.where(col <= row, gw.astype(F32), 0.0)]
where the time goes in v2:
time: 87.2 us; the launch traced here: 86.4 us
  Pallas kernels  78.5 us (90%)
  local copies, waits for them, and re-layouts  5.03 us (6%)
  other arithmetic  2.19 us (3%)
    pallas_call x1, Pallas kernels, per_device(): pl.pallas_call(functools.partial(kernel, chans * X), out_shape=(jax.Shape...  78.5 us
    unnamed x5, local copies, waits for them, and re-layouts  3.65 us
    select_n x1, other arithmetic, per_device(): grad_weight = jnp.where(col <= row, gw.astype(F32), 0.0)  2.18 us

profile of v2, /device:TPU:1, one launch (start us, length us, event | category | flops | bytes accessed | tf_op | source)
XLA Modules:
  0.0 86.4 jit_solution(14865827123812780136)
XLA Ops:
  0.7 78.5 %shard_map.118 = (bf16[128,512]{1,0:T(8,128)(2,1)}, bf16[128,512]{1,0:T(8,128)(2,1)}, f32[8,512]{1,0:T(8,128)}, bf16[128,2048]{1,0:T(8,128)(2,1)}, f32[1,128]{1,0:T(1,128)}) custom-call(bf16[128,512]{1,0:T(8,128)(2,1)} %gate_h.1, bf16[128,512]{1,0:T(8,128)(2,1)} %value_h.1, f32[1,512]{1,0:T(1,128)} %bitcast.8, f32[1,512]{1,0:T(1,128)} %bitcast.9, ...), custom_call_target="tpu_custom_call" | custom-call | tf_op jit(solution)/shard_map/pallas_call | solution.py:477
  79.2 0.0 copy-start
  79.2 1.4 %fusion = (f32[1,512]{1,0:T(1,128)}, f32[1,512]{1,0:T(1,128)}) fusion(f32[8,512]{1,0:T(8,128)} %get-tuple-element.13), kind=kLoop, calls=%fused_computation.3 | loop fusion | bytes 8192 | tf_op jit(solution)/shard_map/slice | solution.py:548
  80.6 2.2 %convert_select_fusion = f32[128,2048]{1,0:T(8,128)} fusion(bf16[128,2048]{1,0:T(8,128)(2,1)} %get-tuple-element.14, s32[2048]{0:T(1024)S(1)} %iota_add_fusion, s32[128]{0:T(128)S(1)} %iota_add_fusion.1), kind=kLoop, calls=%fused_computation | loop fusion | flops 786432 | bytes 1581568 | tf_op jit(solution)/shard_map/jit(_where)/select_n | solution.py:547
  82.7 1.6 %copy.16 = bf16[128,512]{1,0:T(8,128)(2,1)} copy(bf16[128,512]{1,0:T(8,128)(2,1)} %get-tuple-element.24) | data formatting | bytes 262144
  84.3 1.6 %copy.17 = bf16[128,512]{1,0:T(8,128)(2,1)} copy(bf16[128,512]{1,0:T(8,128)(2,1)} %get-tuple-element.25) | data formatting | bytes 262144
  85.9 0.0 copy-done
  85.9 0.5 copy.18
  (2 shorter events, 0.0 us)
Async XLA Ops:
  79.2 6.7 %copy-start = (f32[1,128]{1,0:T(1,128)S(1)}, f32[1,128]{1,0:T(1,128)}, u32[]{:S(2)}) copy-start(f32[1,128]{1,0:T(1,128)} %get-tuple-element.15) | copy-start | bytes 1540

commit v3 on v2

v3 whole, which is shorter than its diff:
```python
import contextlib
import functools

import jax
import jax.numpy as jnp
from jax import lax
from jax.experimental import pallas as pl
from jax.experimental.pallas import tpu as pltpu
from jax.sharding import PartitionSpec as P

MESH = pl.DeviceIdType.MESH
F32 = jnp.float32
BF16 = jnp.bfloat16
T = 128
R = 8
Z = 8
X = 4
Y = 4


def at(name):
    return contextlib.nullcontext()


def dot(a, b, ca, cb):
    return lax.dot_general(a, b, (((ca,), (cb,)), ((), ())), preferred_element_type=F32)


def kernel(
    hidden,
    gate_h, value_h, gain_h, shift_h, w_h, tbias_h, go_h,
    gg_out, gv_out, gs_out, gw_out, tb_out,
    g_all, n_all, wt, s_acc, s_sib, s_send, s_recv, gn_own, gn_send, gn_recv,
    gw_send, gwo, gwx, gwr, gwf,
    stat1, stat2, red1, red2, cen, rows,
    gate, value, gain, shift, w, tbias, go, in_sem,
    gg, gv, gs, tb, out_sem, gw_sem,
    g_ss, g_rs, gb_rs, w_ss, w_rs, f_ss, f_rs, n_ss, n_rs, sb_ss, sb_rs, s_ss, s_rs, gn_ss, gn_rs,
    go_ss, go_rs, gx_ss, gx_rs, gf_ss, gf_rs,
    st_ss, st_rs, sp_ss, sp_rs, ra_ss, ra_rs, rb_ss, rb_rs,
):
    s = lax.axis_index("seq")
    x = lax.axis_index("hid")
    z = s // R
    r = s % R
    y = r // 2
    c = r % 2
    sib = z * R + y * 2 + (1 - c)
    H = R * T // 2

    def rcopy(src, dst, ss, rs, ds, dx):
        return pltpu.make_async_remote_copy(
            src_ref=src, dst_ref=dst, send_sem=ss, recv_sem=rs,
            device_id=(ds, dx), device_id_type=MESH,
        )

    def plane(d):
        q = (r + d) % R
        return q, z * R + q

    def across(e):
        q = (y + e) % Y * 2 + c
        return q, z * R + q

    def chunk(k, core):
        p = (k + core * ((z + 1) // 2)) % (z + 1)
        evens = (z + 2) // 2
        p = z - jnp.where(p < evens, 2 * p, 2 * (p - evens) + 1)
        return jnp.where(k > z, z + 1, p)

    n_shared = jnp.maximum(z - (Z // 2 - 1), 0)
    quarter = pl.ds(pl.multiple_of(x * (T // X), T // X), T // X)

    def shared(k):
        return (k % 2 == 0) & (k < 2 * n_shared)

    def columns(zz, q):
        return pl.ds(pl.multiple_of((zz * R + q) * T, T), T)

    def share_send(m, carry):
        for d in range(1, R):
            q, dev = plane(d)
            zz = chunk(2 * m, q % 2)
            rcopy(
                w.at[quarter, columns(zz, q)], wt.at[zz, r, quarter],
                w_ss.at[2 * m], w_rs.at[zz], dev, x,
            ).start()
        zz = chunk(2 * m, c)
        wt[zz, r, quarter] = w[quarter, columns(zz, r)]
        return carry

    def share_pass(m, carry):
        zz = chunk(2 * m, c)
        got = wt.at[zz, 1:, quarter]
        rcopy(got, got, w_ss.at[zz], w_rs.at[zz], sib, x).wait_recv()
        for d in range(1, X):
            t = (x + d) % X
            part = wt.at[zz, :, quarter]
            rcopy(part, part, f_ss.at[zz], f_rs.at[zz], s, t).start()
        return carry

    loads = [
        pltpu.make_async_copy(a, b, in_sem.at[i])
        for i, (a, b) in enumerate((
            (value_h, value), (go_h, go), (gate_h, gate), (w_h, w),
            (gain_h, gain), (shift_h, shift), (tbias_h, tbias),
        ))
    ]
    for load in loads:
        load.start()

    barrier = pltpu.get_barrier_semaphore()
    for d in range(1, R):
        q, dev = plane(d)
        pl.semaphore_signal(barrier, inc=1, device_id=(dev, x), device_id_type=MESH)
    for d in range(1, Z):
        pl.semaphore_signal(
            barrier, inc=1, device_id=((z + d) % Z * R + r, x), device_id_type=MESH
        )
    for d in range(1, X):
        pl.semaphore_signal(barrier, inc=1, device_id=(s, (x + d) % X), device_id_type=MESH)

    for load in loads[:3]:
        load.wait()
    v = value[...].astype(F32)
    gm = (go[...].astype(F32) * gate[...].astype(F32)).astype(BF16)
    g_all[r] = gm
    lane = lax.broadcasted_iota(jnp.int32, (T, T), 1)

    def as_rows(cols):
        m = jnp.zeros((T, T), F32)
        for i, col in enumerate(cols):
            m = jnp.where(lane == i, col, m)
        return m.T[:8]

    stat1[x] = as_rows((
        jnp.sum(v, axis=1, keepdims=True),
        jnp.sum(v * v, axis=1, keepdims=True),
        jnp.sum(gm.astype(F32), axis=1, keepdims=True),
    ))
    for load in loads[3:]:
        load.wait()
    with at("barrier"):
        pl.semaphore_wait(barrier, (R - 1) + (Z - 1) + (X - 1))

    def x_send(buf, ss, rs):
        for d in range(1, X):
            t = (x + d) % X
            rcopy(buf.at[x], buf.at[x], ss, rs, s, t).start()

    def x_wait(buf, ss, rs):
        cp = rcopy(buf.at[1:], buf.at[1:], ss, rs, sib, x)
        cp.wait_recv()
        cp.wait_send()

    x_send(stat1, st_ss, st_rs)
    lax.fori_loop(0, n_shared, share_send, 0)
    for e in (1, 3, 2):
        q, dev = across(e)
        rcopy(g_all.at[r], g_all.at[r], g_ss, g_rs.at[r], dev, x).start()
    rcopy(g_all.at[r], g_all.at[r], g_ss, gb_rs, sib, x).start()

    def w_send(k, carry):
        @pl.when(jnp.logical_not(shared(k)))
        def _():
            for d in range(1, R):
                q, dev = plane(d)
                zz = chunk(k, q % 2)
                rcopy(
                    w.at[:, columns(zz, q)], wt.at[zz, r], w_ss.at[k], w_rs.at[zz], dev, x
                ).start()

        return carry

    with at("w send"):
        lax.fori_loop(0, z + 1, w_send, 0)

    with at("stat wait"):
        x_wait(stat1, st_ss, st_rs)
    tot = stat1[0] + stat1[1] + stat1[2] + stat1[3]
    tb[...] = tot[2:3]
    colm = jnp.concatenate([tot[:3], tbias[...], jnp.zeros((T - 4, T), F32)], axis=0).T
    mean = colm[:, 0:1] / hidden
    var = colm[:, 1:2] / hidden - mean * mean
    inv = lax.rsqrt(var + 1e-05)
    centred = (v - mean) * inv
    cen[...] = centred
    rows[0] = jnp.broadcast_to(inv, (T, T))
    rows[1] = jnp.broadcast_to(colm[:, 3:4], (T, T))
    n_all[z] = (centred * gain[...] + shift[...]).astype(BF16)

    with at("n send"):
        for d in (1, 7, 2, 6, 3, 5, 4):
            zz = z + d

            @pl.when(zz < Z)
            def _():
                rcopy(n_all.at[z], n_all.at[z], n_ss.at[zz], n_rs.at[z], zz * R + r, x).start()

    with at("share pass"):
        lax.fori_loop(0, n_shared, share_pass, 0)

    with at("g wait"):
        for e in (1, 3, 2):
            q, dev = across(e)
            rcopy(g_all.at[q], g_all.at[q], g_ss, g_rs.at[q], dev, x).wait_recv()
            rcopy(g_all.at[q], g_all.at[q], g_ss, gb_rs, sib, x).start()
        rcopy(g_all.at[Y:], g_all.at[Y:], g_ss, gb_rs, sib, x).wait_recv()

    def arrive(k):
        zz = chunk(k, c)

        @pl.when(shared(k))
        def _():
            with at("share wait"):
                got = wt.at[zz, :, : T - T // X]
                cp = rcopy(got, got, f_ss.at[zz], f_rs.at[zz], sib, x)
                cp.wait_recv()
                cp.wait_send()

        @pl.when(jnp.logical_not(shared(k)) & (k <= z))
        def _():
            with at("w wait"):
                got = wt.at[zz, 1:]
                rcopy(got, got, w_ss.at[zz], w_rs.at[zz], sib, x).wait_recv()
            wt[zz, r] = w[:, columns(zz, r)]

        @pl.when(zz == z)
        def _():
            row = lax.broadcasted_iota(jnp.int32, (T, T), 0)
            own = wt[zz, r].astype(F32)
            wt[zz, r] = jnp.where(row >= lane, own, 0.0).astype(BF16)

            def clear(q, carry):
                wt[zz, q] = jnp.zeros((T, T), BF16)
                return carry

            lax.fori_loop(0, r, clear, 0)

        return zz

    def both(a, b):
        return jnp.concatenate([wt[a].reshape(R * T, T), wt[b].reshape(R * T, T)], axis=1)

    def grad_part(p):
        pair = arrive(2 * p), arrive(2 * p + 1)
        gn = dot(both(*pair), g_all[...].reshape(R * T, -1), 0, 0)
        for i, zz in enumerate(pair):
            part = gn[i * T : (i + 1) * T]

            @pl.when(zz == z)
            def _():
                gn_own[...] = part

            @pl.when(zz < z)
            def _():
                gn_send[zz] = part.astype(BF16)
                rcopy(
                    gn_send.at[zz], gn_recv.at[z], gn_ss.at[zz], gn_rs.at[z], zz * R + r, x
                ).start()

    def half(ref, h):
        return ref.at[pl.ds(pl.multiple_of(h * H, H), H), :]

    def norm_part(p):
        pair = chunk(2 * p, c), chunk(2 * p + 1, c)
        for zz in pair:

            @pl.when(zz < z)
            def _():
                with at("n wait"):
                    rcopy(
                        n_all.at[zz], n_all.at[zz], n_ss.at[zz], n_rs.at[zz], zz * R + r, x
                    ).wait_recv()

        nz = jnp.concatenate([n_all[pair[0]], n_all[pair[1]]], axis=0)
        prod = dot(g_all[...].reshape(R * T, -1), nz, 1, 1).astype(BF16)
        for i, zz in enumerate(pair):
            gw_send[zz] = prod[:, i * T : (i + 1) * T]
            t = zz // 2
            role = (x - t + X) % X

            @pl.when((role == 2) & (zz <= z))
            def _():
                for h, e in ((0, 1), (1, 3)):
                    rcopy(
                        half(gw_send.at[zz], h), gwo.at[zz], go_ss.at[zz, h], go_rs.at[zz],
                        s, (t + e) % X,
                    ).start()

            @pl.when((role % 2 == 1) & (zz <= z))
            def _():
                side = role // 2
                h = 1 - side
                rcopy(
                    half(gw_send.at[zz], h), half(gwx.at[zz % 2, side], h),
                    gx_ss.at[zz, h], gx_rs.at[zz % 2, side, h], s, t,
                ).start()

        sp = dot(both(*pair), nz, 1, 0).reshape(R, T, -1)

        @pl.when(p == 0)
        def _():
            s_acc[...] = sp

        @pl.when(p > 0)
        def _():
            s_acc[...] += sp

    def pass_part(j):
        zz = chunk(j, c)
        t = zz // 2
        role = (x - t + X) % X

        @pl.when((role % 2 == 1) & (zz <= z))
        def _():
            side = role // 2
            with at("gwo wait"):
                rcopy(gwo.at[zz], gwo.at[zz], go_ss.at[zz, 0], go_rs.at[zz], s, t).wait_recv()
            mine = half(gw_send.at[zz], side)
            mine[...] = (mine[...].astype(F32) + gwo[zz].astype(F32)).astype(BF16)
            rcopy(
                mine, half(gwx.at[zz % 2, side], side),
                gx_ss.at[zz, side], gx_rs.at[zz % 2, side, side], s, t,
            ).start()

    @pl.when(z % 2 == 0)
    def _():
        wt[z + 1] = jnp.zeros((R, T, T), BF16)
        n_all[z + 1] = jnp.zeros((T, n_all.shape[2]), BF16)

    pairs = (z + 2) // 2

    def step(k, carry):
        @pl.when(k < pairs)
        def _():
            grad_part(k)

        @pl.when((k >= 1) & (k <= pairs))
        def _():
            norm_part(k - 1)

        @pl.when(k >= 2)
        def _():
            pass_part(2 * (k - 2))
            pass_part(2 * (k - 2) + 1)

        return carry

    lax.fori_loop(0, pairs + 2, step, 0)

    stores = [
        pltpu.make_async_copy(a, b, out_sem.at[i])
        for i, (a, b) in enumerate(((gg, gg_out), (tb, tb_out), (gv, gv_out), (gs, gs_out)))
    ]
    stores[1].start()

    for e in range(Y):
        q = (y + e) % Y
        rcopy(s_acc.at[q * 2 + 1 - c], s_sib.at[q], sb_ss, sb_rs.at[q], sib, x).start()
    def grad_normed():
        def gn_wait(k, carry):
            zz = z + 1 + k
            rcopy(
                gn_send.at[zz], gn_recv.at[zz], gn_ss.at[zz], gn_rs.at[zz], zz * R + r, x
            ).wait_recv()
            gn_own[...] += gn_recv[zz].astype(F32)
            return carry

        with at("gn wait"):
            lax.fori_loop(0, Z - 1 - z, gn_wait, 0)
        gn = gn_own[...]
        centred = cen[...]
        gc = gn * gain[...]
        stat2[x] = as_rows((
            jnp.sum(gc, axis=1, keepdims=True),
            jnp.sum(gc * centred, axis=1, keepdims=True),
        ))
        x_send(stat2, sp_ss, sp_rs)
        red1[r] = jnp.concatenate([
            jnp.sum(gn * centred, axis=0, keepdims=True),
            jnp.sum(gn, axis=0, keepdims=True),
            jnp.zeros((6, gn.shape[1]), F32),
        ], axis=0)
        for d in range(1, R):
            q, dev = plane(d)
            rcopy(red1.at[r], red1.at[r], ra_ss, ra_rs, dev, x).start()
    @pl.when(z >= 6)
    def _():
        grad_normed()

    with at("sib wait"):
        for e in (1, 3, 2, 0):
            q, dev = across(e)
            p = (y + e) % Y
            rcopy(s_acc.at[q], s_sib.at[p], sb_ss, sb_rs.at[p], sib, x).wait_recv()
            if e:
                s_send[p] = (s_acc[q] + s_sib[p]).astype(BF16)
                rcopy(s_send.at[p], s_recv.at[y], s_ss, s_rs.at[y], dev, x).start()

    @pl.when(z < 6)
    def _():
        grad_normed()

    for b in range(2):
        zb = 2 * x + b

        @pl.when(zb <= z)
        def _():
            with at("gwx wait"):
                for side in range(2):
                    for h in range(2):
                        rcopy(
                            half(gw_send.at[zb], h), half(gwx.at[b, side], h),
                            gx_ss.at[zb, h], gx_rs.at[b, side, h], s, (x + 1 + 2 * side) % X,
                        ).wait_recv()
            gwr[b] = (
                gw_send[zb].astype(F32) + gwx[b, 0].astype(F32) + gwx[b, 1].astype(F32)
            ).astype(BF16).reshape(R, T, T)
            for d in range(1, R):
                q, dev = plane(d)
                rcopy(
                    gwr.at[b, q], gwf.at[b, r], gf_ss.at[b], gf_rs.at[b], dev, x
                ).start()
            gwf[b, r] = gwr[b, r]

        @pl.when(zb > z)
        def _():
            gwf[b] = jnp.zeros((R, T, T), BF16)

    with at("red1 wait"):
        cp = rcopy(red1.at[1:], red1.at[1:], ra_ss, ra_rs, sib, x)
        cp.wait_recv()
        cp.wait_send()
    tot = red1[0]
    for q in range(1, R):
        tot = tot + red1[q]
    red2[z] = tot
    for d in range(1, Z):
        zz = (z + d) % Z
        rcopy(red2.at[z], red2.at[z], rb_ss, rb_rs, zz * R + r, x).start()
    acc = s_acc[r] + s_sib[y]
    with at("s wait"):
        for e in (1, 3, 2):
            p = (y + e) % Y
            q, dev = across(e)
            rcopy(s_send.at[p], s_recv.at[p], s_ss, s_rs.at[p], dev, x).wait_recv()
            acc = acc + s_recv[p].astype(F32)
    gg[...] = (go[...].astype(F32) * (acc + rows[1][:, 0:1])).astype(BF16)
    stores[0].start()

    with at("stat2 wait"):
        x_wait(stat2, sp_ss, sp_rs)
    tot = stat2[0] + stat2[1] + stat2[2] + stat2[3]
    colm = jnp.concatenate([tot, jnp.zeros((T - 8, T), F32)], axis=0).T
    centred = cen[...]
    gc = gn_own[...] * gain[...]
    gv[...] = (
        rows[0][:, 0:1] * (gc - colm[:, 0:1] / hidden - centred * (colm[:, 1:2] / hidden))
    ).astype(BF16)
    stores[2].start()


    for b in range(2):
        zb = 2 * x + b

        @pl.when(zb <= z)
        def _():
            with at("gwf wait"):
                cp = rcopy(gwr.at[b, 1:], gwf.at[b, 1:], gf_ss.at[b], gf_rs.at[b], sib, x)
                cp.wait_recv()
                cp.wait_send()

        for q in range(R):
            some = pl.ds((b * R + q) * T, T)
            pltpu.make_async_copy(gwf.at[b, q], gw_out.at[:, some], gw_sem).start()

    rcopy(s_send.at[1:], s_recv.at[1:], s_ss, s_rs.at[0], sib, x).wait_send()
    rcopy(g_all.at[1:], g_all.at[1:], g_ss, gb_rs, sib, x).wait_send()
    rcopy(s_sib, s_sib, sb_ss, sb_rs.at[0], sib, x).wait_send()

    def drain_w(k, carry):
        @pl.when(shared(k))
        def _():
            sent = wt.at[0, 1:, quarter]
            rcopy(sent, sent, w_ss.at[k], w_rs.at[0], sib, x).wait_send()

        @pl.when(jnp.logical_not(shared(k)))
        def _():
            sent = wt.at[0, 1:]
            rcopy(sent, sent, w_ss.at[k], w_rs.at[0], sib, x).wait_send()

        zz = k
        role = (x - zz // 2 + X) % X

        @pl.when(role == 2)
        def _():
            for h in range(2):
                rcopy(
                    half(gw_send.at[zz], h), gwo.at[zz], go_ss.at[zz, h], go_rs.at[zz], s,
                    (x + 1) % X,
                ).wait_send()

        @pl.when(role % 2 == 1)
        def _():
            for h in range(2):
                rcopy(
                    half(gw_send.at[zz], h), half(gwx.at[0, 0], h),
                    gx_ss.at[zz, h], gx_rs.at[0, 0, h], s, (x + 1) % X,
                ).wait_send()

        return carry

    with at("drain"):
        lax.fori_loop(0, z + 1, drain_w, 0)

    def drain_gn(zz, carry):
        rcopy(
            gn_send.at[zz], gn_recv.at[z], gn_ss.at[zz], gn_rs.at[z], zz * R + r, x
        ).wait_send()
        return carry

    lax.fori_loop(0, z, drain_gn, 0)

    def drain_n(zz, carry):
        rcopy(n_all.at[z], n_all.at[z], n_ss.at[zz], n_rs.at[z], zz * R + r, x).wait_send()
        return carry

    lax.fori_loop(z + 1, Z, drain_n, 0)

    with at("red2 wait"):
        cp = rcopy(red2.at[1:], red2.at[1:], rb_ss, rb_rs, sib, x)
        cp.wait_recv()
        cp.wait_send()
    tot = red2[0]
    for q in range(1, Z):
        tot = tot + red2[q]
    gs[...] = tot
    stores[3].start()
    with at("store wait"):
        for store in stores:
            store.wait()
        pltpu.make_async_copy(gwf, gwf, gw_sem).wait()


def finish(
    gg_in, gv_in, gs_in, gw_in, tb_in, gg_out, gv_out, gain_out, shift_out, gw_out, tb_out,
    gg, gv, gs, gw, tb, gw_f, in_sem, sem,
):
    rows, width = gw_f.shape
    loads = [
        pltpu.make_async_copy(a, b, in_sem.at[i])
        for i, (a, b) in enumerate(
            ((gw_in, gw), (gg_in, gg), (gv_in, gv), (gs_in, gs), (tb_in, tb))
        )
    ]
    for load in loads:
        load.start()
    row = lax.axis_index("seq") * rows + lax.broadcasted_iota(jnp.int32, (rows, T), 0)
    lane = lax.axis_index("hid") * width + lax.broadcasted_iota(jnp.int32, (rows, T), 1)
    loads[0].wait()
    copies = []
    for q in range(width // T):
        cols = slice(q * T, (q + 1) * T)
        gw_f[:, cols] = jnp.where(lane + q * T <= row, gw[:, cols].astype(F32), 0.0)
        if q % 4 == 3:
            some = pl.ds((q - 3) * T, 4 * T)
            copies.append(
                pltpu.make_async_copy(gw_f.at[:, some], gw_out.at[:, some], sem.at[5 + q // 4])
            )
            copies[-1].start()
        if q == 3:
            for load in loads[1:]:
                load.wait()
            for i, (a, b) in enumerate((
                (gg, gg_out), (gv, gv_out), (tb, tb_out),
                (gs.at[0:1], gain_out), (gs.at[1:2], shift_out),
            )):
                copies.append(pltpu.make_async_copy(a, b, sem.at[i]))
                copies[-1].start()
    for copy in copies:
        copy.wait()


def per_device(gate_half, value_half, norm_gain, norm_shift, token_weight, token_bias, grad_output):
    rows, chans = gate_half.shape
    cols = token_weight.shape[1]
    width = cols // X
    dma = pltpu.SemaphoreType.DMA
    anywhere = pl.BlockSpec(memory_space=pl.ANY)
    gg, gv, gs, gw, tb = pl.pallas_call(
        functools.partial(kernel, chans * X),
        out_shape=(
            jax.ShapeDtypeStruct((rows, chans), BF16),
            jax.ShapeDtypeStruct((rows, chans), BF16),
            jax.ShapeDtypeStruct((8, chans), F32),
            jax.ShapeDtypeStruct((rows, width), BF16),
            jax.ShapeDtypeStruct((1, rows), F32),
        ),
        in_specs=[anywhere] * 7,
        out_specs=(anywhere,) * 5,
        scratch_shapes=[
            pltpu.VMEM((R, T, chans), BF16),
            pltpu.VMEM((Z, T, chans), BF16),
            pltpu.VMEM((Z, R, T, T), BF16),
            pltpu.VMEM((R, T, chans), F32),
            pltpu.VMEM((Y, T, chans), F32),
            pltpu.VMEM((Y, T, chans), BF16),
            pltpu.VMEM((Y, T, chans), BF16),
            pltpu.VMEM((T, chans), F32),
            pltpu.VMEM((Z, T, chans), BF16),
            pltpu.VMEM((Z, T, chans), BF16),
            pltpu.VMEM((Z, R * T, T), BF16),
            pltpu.VMEM((Z, R * T // 2, T), BF16),
            pltpu.VMEM((2, 2, R * T, T), BF16),
            pltpu.VMEM((2, R, T, T), BF16),
            pltpu.VMEM((2, R, T, T), BF16),
            pltpu.VMEM((X, 8, T), F32),
            pltpu.VMEM((X, 8, T), F32),
            pltpu.VMEM((R, 8, chans), F32),
            pltpu.VMEM((Z, 8, chans), F32),
            pltpu.VMEM((T, chans), F32),
            pltpu.VMEM((2, T, T), F32),
            pltpu.VMEM((rows, chans), BF16),
            pltpu.VMEM((rows, chans), BF16),
            pltpu.VMEM((1, chans), F32),
            pltpu.VMEM((1, chans), F32),
            pltpu.VMEM((rows, cols), BF16),
            pltpu.VMEM((1, rows), F32),
            pltpu.VMEM((rows, chans), BF16),
            dma((7,)),
            pltpu.VMEM((rows, chans), BF16),
            pltpu.VMEM((rows, chans), BF16),
            pltpu.VMEM((8, chans), F32),
            pltpu.VMEM((1, rows), F32),
            dma((4,)), dma(()),
            dma(()), dma((R,)), dma(()),
            dma((Z,)), dma((Z,)),
            dma((Z,)), dma((Z,)),
            dma((Z,)), dma((Z,)),
            dma(()), dma((Y,)),
            dma(()), dma((Y,)),
            dma((Z,)), dma((Z,)),
            dma((Z, 2)), dma((Z,)),
            dma((Z, 2)), dma((2, 2, 2)),
            dma((2,)), dma((2,)),
            *([dma(())] * 8),
        ],
        compiler_params=pltpu.CompilerParams(
            collective_id=0, has_side_effects=True, vmem_limit_bytes=60 * 1024 * 1024
        ),
    )(
        gate_half, value_half, norm_gain[None], norm_shift[None], token_weight, token_bias[None],
        grad_output,
    )
    gg, gv, gain, shift, gw, tb = pl.pallas_call(
        finish,
        out_shape=(
            jax.ShapeDtypeStruct((rows, chans), BF16),
            jax.ShapeDtypeStruct((rows, chans), BF16),
            jax.ShapeDtypeStruct((1, chans), F32),
            jax.ShapeDtypeStruct((1, chans), F32),
            jax.ShapeDtypeStruct((rows, width), F32),
            jax.ShapeDtypeStruct((1, rows), F32),
        ),
        in_specs=[anywhere] * 5,
        out_specs=(anywhere,) * 6,
        scratch_shapes=[
            pltpu.VMEM((rows, chans), BF16),
            pltpu.VMEM((rows, chans), BF16),
            pltpu.VMEM((8, chans), F32),
            pltpu.VMEM((rows, width), BF16),
            pltpu.VMEM((1, rows), F32),
            pltpu.VMEM((rows, width), F32),
            dma((5,)),
            dma((5 + width // T // 4,)),
        ],
        compiler_params=pltpu.CompilerParams(vmem_limit_bytes=60 * 1024 * 1024),
    )(gg, gv, gs, gw, tb)
    return gg, gv, gain[0], shift[0], gw, tb[0]


def solution(mesh):
    placed = (
        P("seq", "hid"),
        P("seq", "hid"),
        P("hid"),
        P("hid"),
        P("seq", None),
        P("seq"),
        P("seq", "hid"),
    )
    return jax.shard_map(
        per_device,
        mesh=mesh,
        in_specs=placed,
        out_specs=(P("seq", "hid"), P("seq", "hid"), P("hid"), P("hid"), P("seq", "hid"), P("seq")),
        check_vma=False,
    )
```

time: 87.2 us -> 70.4 us (0.81)
  the two profiles are of different devices: /device:TPU:1 before, /device:TPU:2 now
where the time goes in v3:
time: 70.4 us; the launch traced here: 70.3 us
  Pallas kernels  69.6 us (99%)
    pallas_call x1, Pallas kernels, per_device(): pl.pallas_call(functools.partial(kernel, chans * X), out_shape=(jax.Shape...  67.4 us
    pallas_call x1, Pallas kernels, per_device(): pl.pallas_call(finish, out_shape=(jax.ShapeDtypeStruct((rows, chans), BF1...  2.26 us

profile of v3, /device:TPU:2, one launch (start us, length us, event | category | flops | bytes accessed | tf_op | source)
XLA Modules:
  0.0 70.3 jit_solution(9968682535426589992)
XLA Ops:
  0.6 67.4 %shard_map.118 = (bf16[128,512]{1,0:T(8,128)(2,1)}, bf16[128,512]{1,0:T(8,128)(2,1)}, f32[8,512]{1,0:T(8,128)}, bf16[128,2048]{1,0:T(8,128)(2,1)}, f32[1,128]{1,0:T(1,128)}) custom-call(bf16[128,512]{1,0:T(8,128)(2,1)} %gate_h.1, bf16[128,512]{1,0:T(8,128)(2,1)} %value_h.1, f32[1,512]{1,0:T(1,128)} %bitcast.6, f32[1,512]{1,0:T(1,128)} %bitcast.7, ...), custom_call_target="tpu_custom_call" | custom-call | tf_op jit(solution)/shard_map/pallas_call | solution.py:591
  68.0 2.3 %shard_map.119 = (bf16[128,512]{1,0:T(8,128)(2,1)}, bf16[128,512]{1,0:T(8,128)(2,1)}, f32[1,512]{1,0:T(1,128)}, f32[1,512]{1,0:T(1,128)}, f32[128,2048]{1,0:T(8,128)}, /*index=5*/f32[1,128]{1,0:T(1,128)}) custom-call(bf16[128,512]{1,0:T(8,128)(2,1)} %get-tuple-element.17.gg_in, bf16[128,512]{1,0:T(8,128)(2,1)} %get-tuple-element.18.gv_in, ...), custom_call_target="tpu_custom_call" | custom-call | tf_op jit(solution)/shard_map/pallas_call | solution.py:656

commit v4 on v3

--- a/solution.py
+++ b/solution.py
@@ -68,7 +68,7 @@
         p = z - jnp.where(p < evens, 2 * p, 2 * (p - evens) + 1)
         return jnp.where(k > z, z + 1, p)
 
-    n_shared = jnp.maximum(z - (Z // 2 - 1), 0)
+    n_shared = jnp.maximum(z - Z // 2, 0)
     quarter = pl.ds(pl.multiple_of(x * (T // X), T // X), T // X)
 
     def shared(k):
@@ -252,9 +252,14 @@
             def _():
                 gn_own[...] = part
 
-            @pl.when(zz < z)
+            far = z - zz
+
+            @pl.when(far > 0)
             def _():
                 gn_send[zz] = part.astype(BF16)
+
+            @pl.when(far >= 1)
+            def _():
                 rcopy(
                     gn_send.at[zz], gn_recv.at[z], gn_ss.at[zz], gn_rs.at[z], zz * R + r, x
                 ).start()
@@ -264,6 +269,7 @@
 
     def norm_part(p):
         pair = chunk(2 * p, c), chunk(2 * p + 1, c)
+
         for zz in pair:
 
             @pl.when(zz < z)
@@ -330,24 +336,29 @@
         n_all[z + 1] = jnp.zeros((T, n_all.shape[2]), BF16)
 
     pairs = (z + 2) // 2
+    lag = jnp.where(z == Z - 1, 1, 2)
 
     def step(k, carry):
         @pl.when(k < pairs)
         def _():
             grad_part(k)
 
-        @pl.when((k >= 1) & (k <= pairs))
-        def _():
-            norm_part(k - 1)
-
-        @pl.when(k >= 2)
-        def _():
-            pass_part(2 * (k - 2))
-            pass_part(2 * (k - 2) + 1)
+        @pl.when((k >= lag) & (k < pairs + lag))
+        def _():
+            norm_part(k - lag)
+
+        @pl.when(k >= lag + 2)
+        def _():
+            pass_pair(k - lag - 2, 0)
 
         return carry
 
-    lax.fori_loop(0, pairs + 2, step, 0)
+    def pass_pair(p, carry):
+        pass_part(2 * p)
+        pass_part(2 * p + 1)
+        return carry
+
+    lax.fori_loop(0, pairs + lag, step, 0)
 
     stores = [
         pltpu.make_async_copy(a, b, out_sem.at[i])
@@ -359,16 +370,17 @@
         q = (y + e) % Y
         rcopy(s_acc.at[q * 2 + 1 - c], s_sib.at[q], sb_ss, sb_rs.at[q], sib, x).start()
     def grad_normed():
-        def gn_wait(k, carry):
-            zz = z + 1 + k
-            rcopy(
-                gn_send.at[zz], gn_recv.at[zz], gn_ss.at[zz], gn_rs.at[zz], zz * R + r, x
-            ).wait_recv()
-            gn_own[...] += gn_recv[zz].astype(F32)
-            return carry
-
         with at("gn wait"):
-            lax.fori_loop(0, Z - 1 - z, gn_wait, 0)
+            for d in range(1, Z):
+                zz = z + d
+
+                @pl.when(zz < Z)
+                def _():
+                    rcopy(
+                        gn_send.at[0], gn_recv.at[zz], gn_ss.at[0], gn_rs.at[zz], sib, x
+                    ).wait_recv()
+                    gn_own[...] += gn_recv[zz].astype(F32)
+
         gn = gn_own[...]
         centred = cen[...]
         gc = gn * gain[...]
@@ -398,35 +410,46 @@
                 s_send[p] = (s_acc[q] + s_sib[p]).astype(BF16)
                 rcopy(s_send.at[p], s_recv.at[y], s_ss, s_rs.at[y], dev, x).start()
 
+    def collect():
+        for b in range(2):
+            zb = 2 * x + b
+
+            @pl.when(zb <= z)
+            def _():
+                with at("gwx wait"):
+                    for side in range(2):
+                        for h in range(2):
+                            rcopy(
+                                half(gw_send.at[zb], h), half(gwx.at[b, side], h),
+                                gx_ss.at[zb, h], gx_rs.at[b, side, h], s, (x + 1 + 2 * side) % X,
+                            ).wait_recv()
+                gwr[b] = (
+                    gw_send[zb].astype(F32) + gwx[b, 0].astype(F32) + gwx[b, 1].astype(F32)
+                ).astype(BF16).reshape(R, T, T)
+                for d in range(1, R):
+                    q, dev = plane(d)
+                    rcopy(
+                        gwr.at[b, q], gwf.at[b, r], gf_ss.at[b], gf_rs.at[b], dev, x
+                    ).start()
+                gwf[b, r] = gwr[b, r]
+
+            @pl.when(zb > z)
+            def _():
+                gwf[b] = jnp.zeros((R, T, T), BF16)
+
+    lax.fori_loop(jnp.maximum(pairs - 2, 0), pairs, pass_pair, 0)
+
+    @pl.when(z < Z // 2)
+    def _():
+        collect()
+
     @pl.when(z < 6)
     def _():
         grad_normed()
 
-    for b in range(2):
-        zb = 2 * x + b
-
-        @pl.when(zb <= z)
-        def _():
-            with at("gwx wait"):
-                for side in range(2):
-                    for h in range(2):
-                        rcopy(
-                            half(gw_send.at[zb], h), half(gwx.at[b, side], h),
-                            gx_ss.at[zb, h], gx_rs.at[b, side, h], s, (x + 1 + 2 * side) % X,
-                        ).wait_recv()
-            gwr[b] = (
-                gw_send[zb].astype(F32) + gwx[b, 0].astype(F32) + gwx[b, 1].astype(F32)
-            ).astype(BF16).reshape(R, T, T)
-            for d in range(1, R):
-                q, dev = plane(d)
-                rcopy(
-                    gwr.at[b, q], gwf.at[b, r], gf_ss.at[b], gf_rs.at[b], dev, x
-                ).start()
-            gwf[b, r] = gwr[b, r]
-
-        @pl.when(zb > z)
-        def _():
-            gwf[b] = jnp.zeros((R, T, T), BF16)
+    @pl.when(z >= Z // 2)
+    def _():
+        collect()
 
     with at("red1 wait"):
         cp = rcopy(red1.at[1:], red1.at[1:], ra_ss, ra_rs, sib, x)
@@ -522,11 +545,11 @@
 
     lax.fori_loop(0, z, drain_gn, 0)
 
-    def drain_n(zz, carry):
-        rcopy(n_all.at[z], n_all.at[z], n_ss.at[zz], n_rs.at[z], zz * R + r, x).wait_send()
-        return carry
-
-    lax.fori_loop(z + 1, Z, drain_n, 0)
+    for d in range(1, Z):
+
+        @pl.when(z + d < Z)
+        def _():
+            rcopy(n_all.at[z], n_all.at[z], n_ss.at[z + d], n_rs.at[z], sib, x).wait_send()
 
     with at("red2 wait"):
         cp = rcopy(red2.at[1:], red2.at[1:], rb_ss, rb_rs, sib, x)

time: 70.4 us -> 65.7 us (0.933)
  the two profiles are of different devices: /device:TPU:2 before, /device:TPU:1 now
where the time goes in v4:
time: 65.7 us; the launch traced here: 65.6 us
  Pallas kernels  64.9 us (99%)
    pallas_call x1, Pallas kernels, per_device(): pl.pallas_call(functools.partial(kernel, chans * X), out_shape=(jax.Shape...  62.7 us
    pallas_call x1, Pallas kernels, per_device(): pl.pallas_call(finish, out_shape=(jax.ShapeDtypeStruct((rows, chans), BF1...  2.26 us

profile of v4, /device:TPU:1, one launch (start us, length us, event | category | flops | bytes accessed | tf_op | source)
XLA Modules:
  0.0 65.6 jit_solution(9956914491263473538)
XLA Ops:
  0.6 62.7 %shard_map.118 = (bf16[128,512]{1,0:T(8,128)(2,1)}, bf16[128,512]{1,0:T(8,128)(2,1)}, f32[8,512]{1,0:T(8,128)}, bf16[128,2048]{1,0:T(8,128)(2,1)}, f32[1,128]{1,0:T(1,128)}) custom-call(bf16[128,512]{1,0:T(8,128)(2,1)} %gate_h.1, bf16[128,512]{1,0:T(8,128)(2,1)} %value_h.1, f32[1,512]{1,0:T(1,128)} %bitcast.6, f32[1,512]{1,0:T(1,128)} %bitcast.7, ...), custom_call_target="tpu_custom_call" | custom-call | tf_op jit(solution)/shard_map/pallas_call | solution.py:614
  63.3 2.3 %shard_map.119 = (bf16[128,512]{1,0:T(8,128)(2,1)}, bf16[128,512]{1,0:T(8,128)(2,1)}, f32[1,512]{1,0:T(1,128)}, f32[1,512]{1,0:T(1,128)}, f32[128,2048]{1,0:T(8,128)}, /*index=5*/f32[1,128]{1,0:T(1,128)}) custom-call(bf16[128,512]{1,0:T(8,128)(2,1)} %get-tuple-element.17.gg_in, bf16[128,512]{1,0:T(8,128)(2,1)} %get-tuple-element.18.gv_in, ...), custom_call_target="tpu_custom_call" | custom-call | tf_op jit(solution)/shard_map/pallas_call | solution.py:679

commit v5 on v4

--- a/solution.py
+++ b/solution.py
@@ -290,7 +290,7 @@
             def _():
                 for h, e in ((0, 1), (1, 3)):
                     rcopy(
-                        half(gw_send.at[zz], h), gwo.at[zz], go_ss.at[zz, h], go_rs.at[zz],
+                        half(gw_send.at[zz], h), gwo.at[zz], go_ss.at[zz], go_rs.at[zz],
                         s, (t + e) % X,
                     ).start()
 
@@ -300,7 +300,7 @@
                 h = 1 - side
                 rcopy(
                     half(gw_send.at[zz], h), half(gwx.at[zz % 2, side], h),
-                    gx_ss.at[zz, h], gx_rs.at[zz % 2, side, h], s, t,
+                    gx_ss.at[zz], gx_rs.at[zz % 2, side, h], s, t,
                 ).start()
 
         sp = dot(both(*pair), nz, 1, 0).reshape(R, T, -1)
@@ -322,12 +322,12 @@
         def _():
             side = role // 2
             with at("gwo wait"):
-                rcopy(gwo.at[zz], gwo.at[zz], go_ss.at[zz, 0], go_rs.at[zz], s, t).wait_recv()
+                rcopy(gwo.at[zz], gwo.at[zz], go_ss.at[zz], go_rs.at[zz], s, t).wait_recv()
             mine = half(gw_send.at[zz], side)
             mine[...] = (mine[...].astype(F32) + gwo[zz].astype(F32)).astype(BF16)
             rcopy(
                 mine, half(gwx.at[zz % 2, side], side),
-                gx_ss.at[zz, side], gx_rs.at[zz % 2, side, side], s, t,
+                gx_ss.at[zz], gx_rs.at[zz % 2, side, side], s, t,
             ).start()
 
     @pl.when(z % 2 == 0)
@@ -392,7 +392,6 @@
         red1[r] = jnp.concatenate([
             jnp.sum(gn * centred, axis=0, keepdims=True),
             jnp.sum(gn, axis=0, keepdims=True),
-            jnp.zeros((6, gn.shape[1]), F32),
         ], axis=0)
         for d in range(1, R):
             q, dev = plane(d)
@@ -421,7 +420,7 @@
                         for h in range(2):
                             rcopy(
                                 half(gw_send.at[zb], h), half(gwx.at[b, side], h),
-                                gx_ss.at[zb, h], gx_rs.at[b, side, h], s, (x + 1 + 2 * side) % X,
+                                gx_ss.at[zb], gx_rs.at[b, side, h], s, (x + 1 + 2 * side) % X,
                             ).wait_recv()
                 gwr[b] = (
                     gw_send[zb].astype(F32) + gwx[b, 0].astype(F32) + gwx[b, 1].astype(F32)
@@ -439,7 +438,7 @@
 
     lax.fori_loop(jnp.maximum(pairs - 2, 0), pairs, pass_pair, 0)
 
-    @pl.when(z < Z // 2)
+    @pl.when(z < 3)
     def _():
         collect()
 
@@ -447,7 +446,7 @@
     def _():
         grad_normed()
 
-    @pl.when(z >= Z // 2)
+    @pl.when(z >= 3)
     def _():
         collect()
 
@@ -518,19 +517,11 @@
 
         @pl.when(role == 2)
         def _():
-            for h in range(2):
-                rcopy(
-                    half(gw_send.at[zz], h), gwo.at[zz], go_ss.at[zz, h], go_rs.at[zz], s,
-                    (x + 1) % X,
-                ).wait_send()
+            rcopy(gw_send.at[0], gw_send.at[0], go_ss.at[zz], go_rs.at[0], sib, x).wait_send()
 
         @pl.when(role % 2 == 1)
         def _():
-            for h in range(2):
-                rcopy(
-                    half(gw_send.at[zz], h), half(gwx.at[0, 0], h),
-                    gx_ss.at[zz, h], gx_rs.at[0, 0, h], s, (x + 1) % X,
-                ).wait_send()
+            rcopy(gw_send.at[0], gw_send.at[0], gx_ss.at[zz], go_rs.at[0], sib, x).wait_send()
 
         return carry
 
@@ -616,7 +607,7 @@
         out_shape=(
             jax.ShapeDtypeStruct((rows, chans), BF16),
             jax.ShapeDtypeStruct((rows, chans), BF16),
-            jax.ShapeDtypeStruct((8, chans), F32),
+            jax.ShapeDtypeStruct((2, chans), F32),
             jax.ShapeDtypeStruct((rows, width), BF16),
             jax.ShapeDtypeStruct((1, rows), F32),
         ),
@@ -640,8 +631,8 @@
             pltpu.VMEM((2, R, T, T), BF16),
             pltpu.VMEM((X, 8, T), F32),
             pltpu.VMEM((X, 8, T), F32),
-            pltpu.VMEM((R, 8, chans), F32),
-            pltpu.VMEM((Z, 8, chans), F32),
+            pltpu.VMEM((R, 2, chans), F32),
+            pltpu.VMEM((Z, 2, chans), F32),
             pltpu.VMEM((T, chans), F32),
             pltpu.VMEM((2, T, T), F32),
             pltpu.VMEM((rows, chans), BF16),
@@ -654,7 +645,7 @@
             dma((7,)),
             pltpu.VMEM((rows, chans), BF16),
             pltpu.VMEM((rows, chans), BF16),
-            pltpu.VMEM((8, chans), F32),
+            pltpu.VMEM((2, chans), F32),
             pltpu.VMEM((1, rows), F32),
             dma((4,)), dma(()),
             dma(()), dma((R,)), dma(()),
@@ -664,8 +655,8 @@
             dma(()), dma((Y,)),
             dma(()), dma((Y,)),
             dma((Z,)), dma((Z,)),
-            dma((Z, 2)), dma((Z,)),
-            dma((Z, 2)), dma((2, 2, 2)),
+            dma((Z,)), dma((Z,)),
+            dma((Z,)), dma((2, 2, 2)),
             dma((2,)), dma((2,)),
             *([dma(())] * 8),
         ],
@@ -691,7 +682,7 @@
         scratch_shapes=[
             pltpu.VMEM((rows, chans), BF16),
             pltpu.VMEM((rows, chans), BF16),
-            pltpu.VMEM((8, chans), F32),
+            pltpu.VMEM((2, chans), F32),
             pltpu.VMEM((rows, width), BF16),
             pltpu.VMEM((1, rows), F32),
             pltpu.VMEM((rows, width), F32),

time: 65.7 us -> 62.4 us (0.950)
  Pallas kernels: 64.9 us -> 61.4 us
    pallas_call x1, Pallas kernels: 62.7 us -> 59.1 us  [per_device(): pl.pallas_call(functools.partial(kernel, chans * X), out_shape=(jax.Shape...]
where the time goes in v5:
time: 62.4 us; the launch traced here: 62 us
  Pallas kernels  61.4 us (98%)
  between operations  0.64 us (1%)
    pallas_call x1, Pallas kernels, per_device(): pl.pallas_call(functools.partial(kernel, chans * X), out_shape=(jax.Shape...  59.1 us
    pallas_call x1, Pallas kernels, per_device(): pl.pallas_call(finish, out_shape=(jax.ShapeDtypeStruct((rows, chans), BF1...  2.26 us

profile of v5, /device:TPU:1, one launch (start us, length us, event | category | flops | bytes accessed | tf_op | source)
XLA Modules:
  0.0 62.0 jit_solution(11146742393600218726)
XLA Ops:
  0.6 59.1 %shard_map.118 = (bf16[128,512]{1,0:T(8,128)(2,1)}, bf16[128,512]{1,0:T(8,128)(2,1)}, f32[2,512]{1,0:T(2,128)}, bf16[128,2048]{1,0:T(8,128)(2,1)}, f32[1,128]{1,0:T(1,128)}) custom-call(bf16[128,512]{1,0:T(8,128)(2,1)} %gate_h.1, bf16[128,512]{1,0:T(8,128)(2,1)} %value_h.1, f32[1,512]{1,0:T(1,128)} %bitcast.6, f32[1,512]{1,0:T(1,128)} %bitcast.7, ...), custom_call_target="tpu_custom_call" | custom-call | tf_op jit(solution)/shard_map/pallas_call | solution.py:605
  59.8 2.3 %shard_map.119 = (bf16[128,512]{1,0:T(8,128)(2,1)}, bf16[128,512]{1,0:T(8,128)(2,1)}, f32[1,512]{1,0:T(1,128)}, f32[1,512]{1,0:T(1,128)}, f32[128,2048]{1,0:T(8,128)}, /*index=5*/f32[1,128]{1,0:T(1,128)}) custom-call(bf16[128,512]{1,0:T(8,128)(2,1)} %get-tuple-element.17.gg_in, bf16[128,512]{1,0:T(8,128)(2,1)} %get-tuple-element.18.gv_in, ...), custom_call_target="tpu_custom_call" | custom-call | tf_op jit(solution)/shard_map/pallas_call | solution.py:670

commit v6 on v5

--- a/solution.py
+++ b/solution.py
@@ -68,6 +68,9 @@
         p = z - jnp.where(p < evens, 2 * p, 2 * (p - evens) + 1)
         return jnp.where(k > z, z + 1, p)
 
+    def first(k):
+        return jnp.where(k > z, z + 1, jnp.where((k < 4) & (z >= 4), (k + z) % 4, k))
+
     n_shared = jnp.maximum(z - Z // 2, 0)
     quarter = pl.ds(pl.multiple_of(x * (T // X), T // X), T // X)
 
@@ -80,17 +83,17 @@
     def share_send(m, carry):
         for d in range(1, R):
             q, dev = plane(d)
-            zz = chunk(2 * m, q % 2)
+            zz = first(2 * m)
             rcopy(
                 w.at[quarter, columns(zz, q)], wt.at[zz, r, quarter],
                 w_ss.at[2 * m], w_rs.at[zz], dev, x,
             ).start()
-        zz = chunk(2 * m, c)
+        zz = first(2 * m)
         wt[zz, r, quarter] = w[quarter, columns(zz, r)]
         return carry
 
     def share_pass(m, carry):
-        zz = chunk(2 * m, c)
+        zz = first(2 * m)
         got = wt.at[zz, 1:, quarter]
         rcopy(got, got, w_ss.at[zz], w_rs.at[zz], sib, x).wait_recv()
         for d in range(1, X):
@@ -165,7 +168,7 @@
         def _():
             for d in range(1, R):
                 q, dev = plane(d)
-                zz = chunk(k, q % 2)
+                zz = first(k)
                 rcopy(
                     w.at[:, columns(zz, q)], wt.at[zz, r], w_ss.at[k], w_rs.at[zz], dev, x
                 ).start()
@@ -208,7 +211,7 @@
         rcopy(g_all.at[Y:], g_all.at[Y:], g_ss, gb_rs, sib, x).wait_recv()
 
     def arrive(k):
-        zz = chunk(k, c)
+        zz = first(k)
 
         @pl.when(shared(k))
         def _():
@@ -303,6 +306,9 @@
                     gx_ss.at[zz], gx_rs.at[zz % 2, side, h], s, t,
                 ).start()
 
+    def mix(p, carry):
+        pair = 2 * p, 2 * p + 1
+        nz = jnp.concatenate([n_all[pair[0]], n_all[pair[1]]], axis=0)
         sp = dot(both(*pair), nz, 1, 0).reshape(R, T, -1)
 
         @pl.when(p == 0)
@@ -312,6 +318,8 @@
         @pl.when(p > 0)
         def _():
             s_acc[...] += sp
+
+        return carry
 
     def pass_part(j):
         zz = chunk(j, c)
@@ -347,7 +355,7 @@
         def _():
             norm_part(k - lag)
 
-        @pl.when(k >= lag + 2)
+        @pl.when((k >= lag + 2) & (z == Z - 1))
         def _():
             pass_pair(k - lag - 2, 0)
 
@@ -359,6 +367,7 @@
         return carry
 
     lax.fori_loop(0, pairs + lag, step, 0)
+    lax.fori_loop(0, pairs, mix, 0)
 
     stores = [
         pltpu.make_async_copy(a, b, out_sem.at[i])
@@ -396,7 +405,7 @@
         for d in range(1, R):
             q, dev = plane(d)
             rcopy(red1.at[r], red1.at[r], ra_ss, ra_rs, dev, x).start()
-    @pl.when(z >= 6)
+    @pl.when(z == Z - 1)
     def _():
         grad_normed()
 
@@ -436,19 +445,15 @@
             def _():
                 gwf[b] = jnp.zeros((R, T, T), BF16)
 
-    lax.fori_loop(jnp.maximum(pairs - 2, 0), pairs, pass_pair, 0)
+    lax.fori_loop(jnp.where(z == Z - 1, pairs - 2, 0), pairs, pass_pair, 0)
 
     @pl.when(z < 3)
     def _():
         collect()
 
-    @pl.when(z < 6)
+    @pl.when(z < Z - 1)
     def _():
         grad_normed()
-
-    @pl.when(z >= 3)
-    def _():
-        collect()
 
     with at("red1 wait"):
         cp = rcopy(red1.at[1:], red1.at[1:], ra_ss, ra_rs, sib, x)
@@ -461,6 +466,10 @@
     for d in range(1, Z):
         zz = (z + d) % Z
         rcopy(red2.at[z], red2.at[z], rb_ss, rb_rs, zz * R + r, x).start()
+    @pl.when(z >= 3)
+    def _():
+        collect()
+
     acc = s_acc[r] + s_sib[y]
     with at("s wait"):
         for e in (1, 3, 2):

time: 62.4 us -> 61.9 us (level)
  Pallas kernels: 61.4 us -> 60.5 us
    pallas_call x1, Pallas kernels: 59.1 us -> 58.3 us  [per_device(): pl.pallas_call(functools.partial(kernel, chans * X), out_shape=(jax.Shape...]
where the time goes in v6:
time: 61.9 us; the launch traced here: 61.2 us
  Pallas kernels  60.5 us (98%)
  between operations  0.64 us (1%)
    pallas_call x1, Pallas kernels, per_device(): pl.pallas_call(functools.partial(kernel, chans * X), out_shape=(jax.Shape...  58.3 us
    pallas_call x1, Pallas kernels, per_device(): pl.pallas_call(finish, out_shape=(jax.ShapeDtypeStruct((rows, chans), BF1...  2.26 us

profile of v6, /device:TPU:1, one launch (start us, length us, event | category | flops | bytes accessed | tf_op | source)
XLA Modules:
  0.0 61.2 jit_solution(8105824433404295644)
XLA Ops:
  0.6 58.3 %shard_map.118 = (bf16[128,512]{1,0:T(8,128)(2,1)}, bf16[128,512]{1,0:T(8,128)(2,1)}, f32[2,512]{1,0:T(2,128)}, bf16[128,2048]{1,0:T(8,128)(2,1)}, f32[1,128]{1,0:T(1,128)}) custom-call(bf16[128,512]{1,0:T(8,128)(2,1)} %gate_h.1, bf16[128,512]{1,0:T(8,128)(2,1)} %value_h.1, f32[1,512]{1,0:T(1,128)} %bitcast.6, f32[1,512]{1,0:T(1,128)} %bitcast.7, ...), custom_call_target="tpu_custom_call" | custom-call | tf_op jit(solution)/shard_map/pallas_call | solution.py:614
  58.9 2.3 %shard_map.119 = (bf16[128,512]{1,0:T(8,128)(2,1)}, bf16[128,512]{1,0:T(8,128)(2,1)}, f32[1,512]{1,0:T(1,128)}, f32[1,512]{1,0:T(1,128)}, f32[128,2048]{1,0:T(8,128)}, /*index=5*/f32[1,128]{1,0:T(1,128)}) custom-call(bf16[128,512]{1,0:T(8,128)(2,1)} %get-tuple-element.17.gg_in, bf16[128,512]{1,0:T(8,128)(2,1)} %get-tuple-element.18.gv_in, ...), custom_call_target="tpu_custom_call" | custom-call | tf_op jit(solution)/shard_map/pallas_call | solution.py:679
